TPU v7x, 32 devices: a 4x4x1 block of a 4x4x8 slice. The times are simulated.
32 devices in a mesh: data: 1 (over z), model: 32 (over y, x, core).
Axes of the slice: x: 4, y: 4, z: 1, core: 2. Of those that a mesh axis runs over, the one named last changes fastest.
The devices are a block of a 4x4x8 slice.
Arguments:
- x_in: bfloat16 [4096, 4096], P(('data', 'model'))
- dy_in: bfloat16 [4096, 4096], P(('data', 'model'))
- w_query: bfloat16 [4096, 32, 128], P(None, 'model')
- w_key: bfloat16 [4096, 128], replicated
- w_value: bfloat16 [4096, 128], replicated
- w_out: bfloat16 [32, 128, 4096], P('model')
Outputs:
- output 1: bfloat16 [4096, 4096], P(('data', 'model'))
- output 2: float32 [4096, 32, 128], P('data', 'model')
- output 3: float32 [4096, 128], P(('data', 'model'))
- output 4: float32 [4096, 128], P(('data', 'model'))
- output 5: float32 [32, 128, 4096], P(('data', 'model'))
All inputs are finite; a program needn't handle non-finite values.
Results may differ from a plain program's by a relative error of at most 0.00898.
Values are sent between devices in bfloat16 or wider.
A program may use at most 768 MiB of HBM per device.

v0:
```python
import math
import jax
import jax.numpy as jnp
from jax import lax
from jax.sharding import PartitionSpec as P


def solution(mesh):
    tok_spec = P(("data", "model"), None)

    def local_step(x_loc, dy_loc, wq_loc, w_key, w_value, wo_loc):
        head_dim = w_key.shape[1]
        score_scale = 1.0 / math.sqrt(head_dim)
        x_full = lax.all_gather(x_loc, "model", axis=0, tiled=True)
        dy_full = lax.all_gather(dy_loc, "model", axis=0, tiled=True)
        key_loc = jnp.dot(x_loc, w_key, preferred_element_type=jnp.float32).astype(jnp.bfloat16)
        value_loc = jnp.dot(x_loc, w_value, preferred_element_type=jnp.float32).astype(jnp.bfloat16)
        keys_all = lax.all_gather(key_loc, "model", axis=0, tiled=True)
        values_all = lax.all_gather(value_loc, "model", axis=0, tiled=True)
        positions = jnp.arange(x_full.shape[0])
        causal = positions[:, None] >= positions[None, :]
        queries = jnp.einsum("td,dhe->the", x_full, wq_loc, preferred_element_type=jnp.float32).astype(jnp.bfloat16)
        scores = jnp.einsum("qhe,ke->hqk", queries, keys_all, preferred_element_type=jnp.float32) * score_scale
        scores = jnp.where(causal[None], scores, -jnp.inf)
        probs_f32 = jax.nn.softmax(scores, axis=-1)
        probs_bf = probs_f32.astype(jnp.bfloat16)
        attn_out = jnp.einsum("hqk,ke->qhe", probs_bf, values_all, preferred_element_type=jnp.float32).astype(jnp.bfloat16)
        dw_out = jnp.einsum("qhe,qd->hed", attn_out, dy_full, preferred_element_type=jnp.float32)
        d_attn = jnp.einsum("qd,hed->qhe", dy_full, wo_loc, preferred_element_type=jnp.float32).astype(jnp.bfloat16)
        d_probs = jnp.einsum("qhe,ke->hqk", d_attn, values_all, preferred_element_type=jnp.float32)
        row_dot = jnp.einsum("qhe,qhe->hq", d_attn, attn_out, preferred_element_type=jnp.float32)
        d_scores = (probs_f32 * (d_probs - row_dot[:, :, None]) * score_scale).astype(jnp.bfloat16)
        d_query = jnp.einsum("hqk,ke->qhe", d_scores, keys_all, preferred_element_type=jnp.float32).astype(jnp.bfloat16)
        dk_part = jnp.einsum("hqk,qhe->ke", d_scores, queries, preferred_element_type=jnp.float32)
        dv_part = jnp.einsum("hqk,qhe->ke", probs_bf, d_attn, preferred_element_type=jnp.float32)
        d_keys = lax.psum_scatter(dk_part, "model", scatter_dimension=0, tiled=True).astype(jnp.bfloat16)
        d_values = lax.psum_scatter(dv_part, "model", scatter_dimension=0, tiled=True).astype(jnp.bfloat16)
        dw_query = jnp.einsum("td,the->dhe", x_full, d_query, preferred_element_type=jnp.float32)
        dx_part = jnp.einsum("the,dhe->td", d_query, wq_loc, preferred_element_type=jnp.float32)
        dx_sum = lax.psum_scatter(dx_part, "model", scatter_dimension=0, tiled=True)
        dx_sum = dx_sum + jnp.einsum("te,de->td", d_keys, w_key, preferred_element_type=jnp.float32)
        dx_sum = dx_sum + jnp.einsum("te,de->td", d_values, w_value, preferred_element_type=jnp.float32)
        dwk_part = jnp.einsum("td,te->de", x_loc, d_keys, preferred_element_type=jnp.float32)
        dwv_part = jnp.einsum("td,te->de", x_loc, d_values, preferred_element_type=jnp.float32)
        dw_key = lax.psum_scatter(dwk_part, "model", scatter_dimension=0, tiled=True)
        dw_value = lax.psum_scatter(dwv_part, "model", scatter_dimension=0, tiled=True)
        return (dx_sum.astype(jnp.bfloat16), dw_query, dw_key, dw_value, dw_out)

    return jax.shard_map(local_step, mesh=mesh, in_specs=(tok_spec, tok_spec, P(None, "model", None), P(None, None), P(None, None), P("model", None, None)), out_specs=(tok_spec, P("data", "model", None), tok_spec, tok_spec, P(("data", "model"), None, None)), check_vma=False)
```

profile of v0, /device:TPU:97, one launch (start us, length us, event | category | flops | bytes accessed | tf_op | source)
XLA Modules:
  0.0 924.0 jit_solution(16820499737997758927)
XLA Ops:
  7.2 0.1 all-gather.7.cloned.1.call-start
  7.3 0.7 all-gather.7.cloned.1.call-update
  8.0 0.1 all-gather.5.cloned.1.call-start
  8.1 2.6 convolution_convert_fusion.3
  10.6 0.1 all-gather.5.cloned.1.call-update
  10.7 0.1 all-gather.11.cloned.1.call-start
  10.8 0.7 all-gather.11.cloned.1.call-update
  11.5 0.1 all-gather.9.cloned.1.call-start
  11.6 2.6 convolution_convert_fusion.2
  14.2 0.1 all-gather.9.cloned.1.call-update
  14.2 0.1 reduce-scatter.10.cloned.1.call-start
  14.3 108.3 %all-gather.7.cloned.1.call-done = bf16[4096,4096]{1,0:T(8,128)(2,1)} async-done(((bf16[128,4096]{1,0:T(8,128)(2,1)}), bf16[4096,4096]{1,0:T(8,128)(2,1)}) %all-gather.7.cloned.1.call-update) | async-done | bytes 33554448 | tf_op jit(solution)/shard_map/all_gather | solution.py:14
  122.6 15.2 %convolution_convert_fusion.1 = bf16[4096,128]{1,0:T(8,128)(2,1)S(1)} fusion(bf16[4096,4096]{1,0:T(8,128)(2,1)} %all-gather.7.cloned.1.call-done, bf16[4096,1,128]{2,0,1:T(8,128)(2,1)S(1)} %copy-done), kind=kOutput, calls=%fused_computation.29 | convolution fusion | flops 4295491584 | bytes 35651584 | tf_op jit(solution)/shard_map/td,dhe->the/dot_general | solution.py:22
  137.9 24.1 %all-gather.5.cloned.1.call-done = bf16[4096,128]{1,0:T(8,128)(2,1)} async-done(((bf16[128,128]{1,0:T(8,128)(2,1)}), bf16[4096,128]{1,0:T(8,128)(2,1)}) %all-gather.5.cloned.1.call-update) | async-done | bytes 1048592 | tf_op jit(solution)/shard_map/all_gather | solution.py:18
  161.9 24.7 %fusion.4 = (f32[4096]{0:T(1024)S(1)}, f32[4096,4096]{1,0:T(8,128)}) fusion(bf16[4096,128]{1,0:T(8,128)(2,1)} %all-gather.5.cloned.1.call-done, bf16[4096,128]{1,0:T(8,128)(2,1)S(1)} %convolution_convert_fusion.1), kind=kOutput, calls=%fused_computation.9 | convolution fusion | flops 4362072064 | bytes 69222400 | tf_op jit(solution)/shard_map/qhe,ke->hqk/dot_general | solution.py:23
  186.6 21.7 %fusion.3 = f32[4096]{0:T(1024)S(1)} fusion(f32[4096,4096]{1,0:T(8,128)} %get-tuple-element.11, f32[4096]{0:T(1024)S(1)} %get-tuple-element.10), kind=kLoop, calls=%fused_computation.8 | loop fusion | flops 83881984 | bytes 67141632 | tf_op jit(solution)/shard_map/reduce_sum | solution.py:25
  208.4 63.2 %all-gather.11.cloned.1.call-done = bf16[4096,4096]{1,0:T(8,128)(2,1)} async-done(((bf16[128,4096]{1,0:T(8,128)(2,1)}), bf16[4096,4096]{1,0:T(8,128)(2,1)}) %all-gather.11.cloned.1.call-update) | async-done | bytes 33554448 | tf_op jit(solution)/shard_map/all_gather | solution.py:15
  271.6 15.6 %convolution_convert_fusion = bf16[4096,128]{1,0:T(8,128)(2,1)S(1)} fusion(bf16[4096,4096]{1,0:T(8,128)(2,1)} %all-gather.11.cloned.1.call-done, bf16[1,128,4096]{2,1,0:T(8,128)(2,1)S(1)} %copy-done.7), kind=kOutput, calls=%fused_computation.28 | convolution fusion | flops 4295491584 | bytes 35651584 | tf_op jit(solution)/shard_map/qd,hed->qhe/dot_general | solution.py:29
  287.3 30.0 %fusion.9 = f32[4096,128]{1,0:T(8,128)} fusion(bf16[4096,128]{1,0:T(8,128)(2,1)S(1)} %convolution_convert_fusion, f32[4096]{0:T(1024)S(1)} %fusion.3, f32[4096]{0:T(1024)S(1)} %get-tuple-element.10, f32[4096,4096]{1,0:T(8,128)} %get-tuple-element.11), kind=kOutput, calls=%fused_computation.14 | convolution fusion | flops 4395630592 | bytes 70287360 | tf_op jit(solution)/shard_map/hqk,qhe->ke/dot_general | solution.py:35
  317.3 1.6 copy.17
  318.9 0.1 reduce-scatter.10.cloned.1.call-update
  319.0 0.1 reduce-scatter.8.cloned.1.call-start
  319.1 0.0 all-gather.9.cloned.1.call-done
  319.1 28.1 %multiply_reduce_fusion = (f32[4096]{0:T(1024)S(1)}, bf16[4096,128]{0,1:T(8,128)(2,1)}) fusion(f32[4096,128]{0,1:T(8,128)S(1)} %copy.17, bf16[4096,128]{1,0:T(8,128)(2,1)} %all-gather.9.cloned.1.call-done, f32[4096]{0:T(1024)S(1)} %fusion.3, f32[4096]{0:T(1024)S(1)} %get-tuple-element.10, f32[4096,4096]{1,0:T(8,128)} %get-tuple-element.11), kind=kOutput, calls=%fused_computation.32 | convolution fusion | flops 4397723648 | bytes 71352320 | tf_op jit(solution)/shard_map/hqk,ke->qhe/dot_general | solution.py:27
  347.2 42.6 %fusion.1 = bf16[1,4096,4096]{1,2,0:T(8,128)(2,1)} fusion(bf16[4096,128]{1,0:T(8,128)(2,1)} %all-gather.9.cloned.1.call-done, bf16[4096,128]{1,0:T(8,128)(2,1)} %copy-done.4, f32[4096]{0:T(1024)S(1)} %get-tuple-element.12, f32[4096]{0:T(1024)S(1)} %fusion.3, f32[4096]{0:T(1024)S(1)} %get-tuple-element.10, f32[4096,4096]{1,0:T(8,128)} %get-tuple-element.11), kind=kOutput, calls=%fused_computation.3 | convolution fusion | flops 4445962240 | bytes 102809600 | tf_op jit(solution)/shard_map/qhe,ke->hqk/dot_general | solution.py:30
  389.8 16.5 %fusion.5 = f32[4096,128]{1,0:T(8,128)} fusion(bf16[4096,128]{1,0:T(8,128)(2,1)} %copy-done.8, bf16[1,4096,4096]{1,2,0:T(8,128)(2,1)} %fusion.1), kind=kOutput, calls=%fused_computation.10 | convolution fusion | flops 4294967296 | bytes 36700160 | tf_op jit(solution)/shard_map/hqk,qhe->ke/dot_general | solution.py:34
  406.3 0.1 reduce-scatter.8.cloned.1.call-update
  406.4 0.1 reduce-scatter.14.cloned.1.call-start
  406.5 0.0 reduce-scatter.10.cloned.1.call-done
  406.5 2.7 convolution_bitcast_fusion.1
  409.2 0.1 reduce-scatter.14.cloned.1.call-update
  409.3 0.1 reduce-scatter.12.cloned.1.call-start
  409.3 65.7 %reduce-scatter.8.cloned.1.call-done = f32[128,128]{1,0:T(8,128)} async-done(((f32[4096,128]{1,0:T(8,128)}), f32[128,128]{1,0:T(8,128)}) %reduce-scatter.8.cloned.1.call-update) | async-done | bytes 65552 | tf_op jit(solution)/shard_map/reduce_scatter | solution.py:36
  475.0 2.6 convolution_bitcast_fusion.2
  477.7 0.1 reduce-scatter.12.cloned.1.call-update
  477.7 0.1 reduce-scatter.6.cloned.1.call-start
  477.8 13.1 %fusion.21 = bf16[4096,128]{0,1:T(8,128)(2,1)S(1)} fusion(bf16[4096,128]{1,0:T(8,128)(2,1)S(1)} %copy-done.3, bf16[1,4096,4096]{1,2,0:T(8,128)(2,1)} %fusion.1), kind=kOutput, calls=%fused_computation.30 | convolution fusion | flops 4295491584 | bytes 35651584 | tf_op jit(solution)/shard_map/hqk,ke->qhe/dot_general | solution.py:33
  490.9 23.1 %fusion.28 = f32[4096,4096]{1,0:T(8,128)} fusion(bf16[4096,128]{0,1:T(8,128)(2,1)S(1)} %fusion.21, bf16[4096,1,128]{2,0,1:T(8,128)(2,1)S(1)} %copy-done), kind=kOutput, calls=%fused_computation.36 | convolution fusion | flops 4294967296 | bytes 69206016 | tf_op jit(solution)/shard_map/the,dhe->td/dot_general | solution.py:39
  514.0 0.1 reduce-scatter.6.cloned.1.call-update
  514.1 14.3 %convolution_bitcast_fusion.3 = f32[4096,1,128]{0,2,1:T(8,128)} fusion(bf16[4096,128]{0,1:T(8,128)(2,1)S(1)} %fusion.21, bf16[4096,4096]{1,0:T(8,128)(2,1)} %all-gather.7.cloned.1.call-done), kind=kOutput, calls=%fused_computation.22 | convolution fusion | flops 4294967296 | bytes 36700160 | tf_op jit(solution)/shard_map/td,the->dhe/dot_general | solution.py:38
  528.4 5.9 copy.11
  534.3 16.7 %convolution_bitcast_fusion = f32[1,128,4096]{2,1,0:T(8,128)} fusion(bf16[4096,128]{0,1:T(8,128)(2,1)} %get-tuple-element.13, bf16[4096,4096]{1,0:T(8,128)(2,1)} %all-gather.11.cloned.1.call-done), kind=kOutput, calls=%fused_computation.19 | convolution fusion | flops 4294967296 | bytes 36700160 | tf_op jit(solution)/shard_map/qhe,qd->hed/dot_general | solution.py:28
  551.0 1.6 copy.13
  552.6 70.5 %reduce-scatter.12.cloned.1.call-done = f32[128,128]{0,1:T(8,128)} async-done(((f32[4096,128]{0,1:T(8,128)}), f32[128,128]{0,1:T(8,128)}) %reduce-scatter.12.cloned.1.call-update) | async-done | bytes 65552 | tf_op jit(solution)/shard_map/reduce_scatter | solution.py:45
  623.1 1.6 copy.12
  624.7 287.7 %reduce-scatter.6.cloned.1.call-done = f32[128,4096]{1,0:T(8,128)} async-done(((f32[4096,4096]{1,0:T(8,128)}), f32[128,4096]{1,0:T(8,128)}) %reduce-scatter.6.cloned.1.call-update) | async-done | bytes 2097168 | tf_op jit(solution)/shard_map/reduce_scatter | solution.py:40
  912.4 2.0 convolution_add_fusion.1
  914.4 2.6 fusion.14
  (19 shorter events, 0.0 us)
Async XLA Ops:
  7.2 115.5 %copy-start = (bf16[4096,1,128]{2,0,1:T(8,128)(2,1)S(1)}, bf16[4096,1,128]{2,0,1:T(8,128)(2,1)}, u32[]{:S(2)}) copy-start(bf16[4096,1,128]{2,0,1:T(8,128)(2,1)} %param.8) | copy-start | bytes 3145732
  7.2 115.4 %all-gather.7.cloned.1.call-start = ((), (), s32[]{:S(2)}) async-start(), calls=%async_computation.6 | async-start | bytes 34603008 | tf_op jit(solution)/shard_map/all_gather | solution.py:14
  8.0 154.0 %all-gather.5.cloned.1.call-start = ((), (), s32[]{:S(2)}) async-start(), calls=%async_computation.5 | async-start | bytes 1081344 | tf_op jit(solution)/shard_map/all_gather | solution.py:18
  10.7 260.9 %all-gather.11.cloned.1.call-start = ((), (), s32[]{:S(2)}) async-start(), calls=%async_computation.8 | async-start | bytes 34603008 | tf_op jit(solution)/shard_map/all_gather | solution.py:15
  11.5 307.6 %all-gather.9.cloned.1.call-start = ((), (), s32[]{:S(2)}) async-start(), calls=%async_computation.7 | async-start | bytes 1081344 | tf_op jit(solution)/shard_map/all_gather | solution.py:19
  14.2 392.3 %reduce-scatter.10.cloned.1.call-start = ((), (), s32[]{:S(2)}) async-start(), calls=%async_computation.11 | async-start | bytes 2162688 | tf_op jit(solution)/shard_map/reduce_scatter | solution.py:37
  137.8 70.5 %copy-start.8 = (bf16[4096,128]{1,0:T(8,128)(2,1)}, bf16[4096,128]{1,0:T(8,128)(2,1)S(1)}, u32[]{:S(2)}) copy-start(bf16[4096,128]{1,0:T(8,128)(2,1)S(1)} %convolution_convert_fusion.1) | copy-start | bytes 3145732
  137.8 133.8 %copy-start.7 = (bf16[1,128,4096]{2,1,0:T(8,128)(2,1)S(1)}, bf16[1,128,4096]{2,1,0:T(8,128)(2,1)}, u32[]{:S(2)}) copy-start(bf16[1,128,4096]{2,1,0:T(8,128)(2,1)} %param.11) | copy-start | bytes 3145732
  287.3 30.0 %copy-start.4 = (bf16[4096,128]{1,0:T(8,128)(2,1)}, bf16[4096,128]{1,0:T(8,128)(2,1)S(1)}, u32[]{:S(2)}) copy-start(bf16[4096,128]{1,0:T(8,128)(2,1)S(1)} %convolution_convert_fusion) | copy-start | bytes 3145732
  319.0 156.1 %reduce-scatter.8.cloned.1.call-start = ((), (), s32[]{:S(2)}) async-start(), calls=%async_computation.10 | async-start | bytes 2162688 | tf_op jit(solution)/shard_map/reduce_scatter | solution.py:36
  347.2 59.3 %copy-start.1 = (bf16[128,4096]{1,0:T(8,128)(2,1)S(1)}, bf16[128,4096]{1,0:T(8,128)(2,1)}, u32[]{:S(2)}) copy-start(bf16[128,4096]{1,0:T(8,128)(2,1)} %param.6) | copy-start | bytes 3145732
  347.2 130.6 %copy-start.3 = (bf16[4096,128]{1,0:T(8,128)(2,1)S(1)}, bf16[4096,128]{1,0:T(8,128)(2,1)}, u32[]{:S(2)}) copy-start(bf16[4096,128]{1,0:T(8,128)(2,1)} %all-gather.5.cloned.1.call-done) | copy-start | bytes 3145732
  406.4 144.6 %reduce-scatter.14.cloned.1.call-start = ((), (), s32[]{:S(2)}) async-start(), calls=%async_computation.13 | async-start | bytes 2162688 | tf_op jit(solution)/shard_map/reduce_scatter | solution.py:46
  409.3 213.9 %reduce-scatter.12.cloned.1.call-start = ((), (), s32[]{:S(2)}) async-start(), calls=%async_computation.12 | async-start | bytes 2162688 | tf_op jit(solution)/shard_map/reduce_scatter | solution.py:45
  477.7 434.6 %reduce-scatter.6.cloned.1.call-start = ((), (), s32[]{:S(2)}) async-start(), calls=%async_computation.9 | async-start | bytes 69206016 | tf_op jit(solution)/shard_map/reduce_scatter | solution.py:40
  514.0 398.3 %copy-start.2 = (bf16[4096,128]{1,0:T(8,128)(2,1)S(1)}, bf16[4096,128]{1,0:T(8,128)(2,1)}, u32[]{:S(2)}) copy-start(bf16[4096,128]{1,0:T(8,128)(2,1)} %param.9) | copy-start | bytes 3145732
  514.0 398.3 %copy-start.6 = (f32[128,128]{1,0:T(8,128)S(1)}, f32[128,128]{1,0:T(8,128)}, u32[]{:S(2)}) copy-start(f32[128,128]{1,0:T(8,128)} %reduce-scatter.8.cloned.1.call-done) | copy-start | bytes 196612
  514.0 400.3 %copy-start.5 = (f32[128,128]{1,0:T(8,128)S(1)}, f32[128,128]{1,0:T(8,128)}, u32[]{:S(2)}) copy-start(f32[128,128]{1,0:T(8,128)} %reduce-scatter.10.cloned.1.call-done) | copy-start | bytes 196612
Sparse Core Ops, SparseCore 0:
  10.1 112.4 all-gather.6
  125.3 36.6 all-gather.4
  164.0 107.5 all-gather.10
  274.1 36.6 all-gather.8
  319.1 68.4 reduce-scatter.9
  406.5 68.4 reduce-scatter.7
  478.4 70.6 reduce-scatter.13
  552.5 70.6 reduce-scatter.11
  627.0 285.3 reduce-scatter.5
where the time goes:
time: 932 us; the launch traced here: 924 us
  waiting for transfers between devices  621 us (67%)
  matrix products  255 us (27%)
  other arithmetic  21.7 us (2%)
  between operations  14.4 us (2%)
  local copies, waits for them, and re-layouts  10.7 us (1%)
    reduce_scatter x1, waiting for transfers between devices, local_step(): dx_sum = lax.psum_scatter(dx_part, 'model', scatter_dimension=0, tiled=True)  288 us
    all_gather x1, waiting for transfers between devices, local_step(): x_full = lax.all_gather(x_loc, 'model', axis=0, tiled=True)  108 us
    reduce_scatter x1, waiting for transfers between devices, local_step(): lax.psum_scatter(dwk_part, 'model', scatter_dimension=0, tiled=True)  70.5 us
    reduce_scatter x1, waiting for transfers between devices, local_step(): lax.psum_scatter(dk_part, 'model', scatter_dimension=0, tiled=True)  65.7 us
    all_gather x1, waiting for transfers between devices, local_step(): dy_full = lax.all_gather(dy_loc, 'model', axis=0, tiled=True)  63.2 us
    dot_general x1, matrix products, local_step(): jnp.einsum('qhe,ke->hqk', d_attn, values_all, preferred_element_type=jnp....  42.6 us
    dot_general x1, matrix products, local_step(): jnp.einsum('hqk,qhe->ke', probs_bf, d_attn, preferred_element_type=jnp.fl...  30 us
    dot_general x1, matrix products, local_step(): jnp.einsum('hqk,ke->qhe', probs_bf, values_all, preferred_element_type=jn...  28.1 us
  transfers between devices with their start and end apart: 9, of which 6 were waited for; matrix products, arithmetic and copies ran while one was open for 31% of the time, Pallas kernels for 0%

commit v1 on v0

v1 whole, which is shorter than its diff:
```python
import functools
import math
import jax
import jax.numpy as jnp
from jax import lax
from jax.experimental import pallas as pl
from jax.experimental.pallas import tpu as pltpu
from jax.sharding import PartitionSpec as P

BLK = 512
F32 = jnp.float32
BF16 = jnp.bfloat16


def _dot(a, b):
    return jnp.dot(a, b, preferred_element_type=F32)


def _flip(a):
    return jnp.transpose(a.astype(F32))


def _fwd_kernel(scale, q_ref, k_ref, vt_ref, o_ref, st_ref, s_ref):
    i = pl.program_id(0)
    qt = _flip(q_ref[...]).astype(BF16)

    def score(j, m8, diag):
        s = _dot(k_ref[pl.ds(pl.multiple_of(j * BLK, BLK), BLK), :], qt) * scale
        if diag:
            key = lax.broadcasted_iota(jnp.int32, (BLK, BLK), 0)
            qry = lax.broadcasted_iota(jnp.int32, (BLK, BLK), 1)
            s = jnp.where(qry >= key, s, -jnp.inf)
        s_ref[j] = s
        return jnp.maximum(m8, jnp.max(s.reshape(BLK // 8, 8, BLK), axis=0))

    m8 = jnp.full((8, BLK), -jnp.inf, F32)
    m8 = lax.fori_loop(0, i, lambda j, c: score(j, c, False), m8)
    m8 = score(i, m8, True)
    m = jnp.max(m8, axis=0, keepdims=True)

    def expo(j, l8):
        p = jnp.exp(s_ref[j] - m)
        s_ref[j] = p
        return l8 + jnp.sum(p.reshape(BLK // 8, 8, BLK), axis=0)

    l8 = lax.fori_loop(0, i + 1, expo, jnp.zeros((8, BLK), F32))
    r = 1.0 / jnp.sum(l8, axis=0, keepdims=True)

    def attend(j, ot):
        return ot + _dot(vt_ref[j], (s_ref[j] * r).astype(BF16))

    ot = lax.fori_loop(0, i + 1, attend, jnp.zeros((o_ref.shape[1], BLK), F32))
    o_ref[...] = jnp.transpose(ot).astype(BF16)
    row = lax.broadcasted_iota(jnp.int32, (8, BLK), 0)
    st_ref[...] = jnp.where(row == 0, m, r)


def _bwd_kernel(scale, q_ref, do_ref, o_ref, st_ref, k_ref, v_ref, kt_ref, dq_ref, dkv_ref):
    i = pl.program_id(0)
    hd = q_ref.shape[1]

    @pl.when(i == 0)
    def _():
        dkv_ref[...] = jnp.zeros_like(dkv_ref)

    qt = _flip(q_ref[...]).astype(BF16)
    dot_f = _flip(do_ref[...])
    c = jnp.sum(dot_f * _flip(o_ref[...]), axis=0, keepdims=True)
    dot_b = dot_f.astype(BF16)
    m = st_ref[0:1, :]
    r = st_ref[1:2, :]

    def step(j, dqt, diag):
        rows = pl.ds(pl.multiple_of(j * BLK, BLK), BLK)
        s = _dot(k_ref[rows, :], qt) * scale
        if diag:
            key = lax.broadcasted_iota(jnp.int32, (BLK, BLK), 0)
            qry = lax.broadcasted_iota(jnp.int32, (BLK, BLK), 1)
            s = jnp.where(qry >= key, s, -jnp.inf)
        p = jnp.exp(s - m) * r
        dp = _dot(v_ref[rows, :], dot_b)
        g = (p * (dp - c) * scale).astype(BF16)
        dkv_ref[rows, 0:hd] += _dot(g, q_ref[...])
        dkv_ref[rows, hd : 2 * hd] += _dot(p.astype(BF16), do_ref[...])
        return dqt + _dot(kt_ref[j], g)

    dqt = jnp.zeros((hd, BLK), F32)
    dqt = lax.fori_loop(0, i, lambda j, a: step(j, a, False), dqt)
    dqt = step(i, dqt, True)
    dq_ref[...] = jnp.transpose(dqt).astype(BF16)


def _attn_fwd(q, k, vt, scale):
    t, hd = q.shape
    n = t // BLK
    return pl.pallas_call(
        functools.partial(_fwd_kernel, scale),
        grid=(n,),
        in_specs=[
            pl.BlockSpec((BLK, hd), lambda i: (i, 0)),
            pl.BlockSpec((t, hd), lambda i: (0, 0)),
            pl.BlockSpec((n, hd, BLK), lambda i: (0, 0, 0)),
        ],
        out_specs=[pl.BlockSpec((BLK, hd), lambda i: (i, 0)), pl.BlockSpec((8, BLK), lambda i: (0, i))],
        out_shape=[jax.ShapeDtypeStruct((t, hd), BF16), jax.ShapeDtypeStruct((8, t), F32)],
        scratch_shapes=[pltpu.VMEM((n, BLK, BLK), F32)],
        compiler_params=pltpu.CompilerParams(vmem_limit_bytes=40 * 2**20),
        cost_estimate=pl.CostEstimate(flops=40 * 10**9, bytes_accessed=8 * t * hd, transcendentals=t * t // 2),
        name="attn_fwd",
    )(q, k, vt)


def _attn_bwd(q, do, o, st, k, v, kt, scale):
    t, hd = q.shape
    n = t // BLK
    blk = pl.BlockSpec((BLK, hd), lambda i: (i, 0))
    whole = pl.BlockSpec((t, hd), lambda i: (0, 0))
    return pl.pallas_call(
        functools.partial(_bwd_kernel, scale),
        grid=(n,),
        in_specs=[
            blk, blk, blk,
            pl.BlockSpec((8, BLK), lambda i: (0, i)),
            whole, whole,
            pl.BlockSpec((n, hd, BLK), lambda i: (0, 0, 0)),
        ],
        out_specs=[blk, pl.BlockSpec((t, 2 * hd), lambda i: (0, 0))],
        out_shape=[jax.ShapeDtypeStruct((t, hd), BF16), jax.ShapeDtypeStruct((t, 2 * hd), F32)],
        compiler_params=pltpu.CompilerParams(vmem_limit_bytes=40 * 2**20),
        cost_estimate=pl.CostEstimate(flops=60 * 10**9, bytes_accessed=16 * t * hd, transcendentals=t * t // 2),
        name="attn_bwd",
    )(q, do, o, st, k, v, kt)


def _tail_kernel(n, dq_ref, dkv_ref, dqa_ref, all_ref, pbuf, sbuf, rbuf, q_sem, p_sem, r_sem, g_sem, f_sem, e_sem, l_sem):
    me = lax.axis_index("model")
    core = lax.rem(me, 2)
    chip = me // 2
    nc = n // 2
    other = 1 - core
    partner = me + 1 - 2 * core
    blk = dkv_ref.shape[2]

    def dev(idx):
        return {"model": idx}

    barrier = pltpu.get_barrier_semaphore()

    @pl.loop(1, n)
    def _(o):
        pl.semaphore_signal(barrier, inc=1, device_id=dev(lax.rem(me + o, n)), device_id_type=pl.DeviceIdType.MESH)

    pl.semaphore_wait(barrier, n - 1)

    pair = pltpu.make_async_remote_copy(
        dkv_ref.at[:, other], pbuf, p_sem.at[0], p_sem.at[1], device_id=dev(partner), device_id_type=pl.DeviceIdType.MESH)
    pair.start()

    def q_copy(o):
        peer = lax.rem(me + o, n)
        return pltpu.make_async_remote_copy(
            dq_ref.at[peer], dqa_ref.at[me], q_sem.at[0, o], q_sem.at[1, o], device_id=dev(peer), device_id_type=pl.DeviceIdType.MESH)

    @pl.loop(1, n)
    def _(o):
        q_copy(o).start()

    mine = pltpu.make_async_copy(dq_ref.at[me], dqa_ref.at[me], l_sem)
    mine.start()
    pair.wait()

    def r_copy(o):
        peer = lax.rem(chip + o, nc) * 2 + core
        return pltpu.make_async_remote_copy(
            sbuf.at[o], rbuf.at[o], r_sem.at[0, o], r_sem.at[1, o], device_id=dev(peer), device_id_type=pl.DeviceIdType.MESH)

    @pl.loop(1, nc)
    def _(o):
        t = lax.rem(chip + o, nc)
        sbuf[o] = dkv_ref[t, core] + pbuf[t]
        r_copy(o).start()

    rbuf[0] = dkv_ref[chip, core] + pbuf[chip]

    @pl.loop(1, nc)
    def _(o):
        r_copy(o).wait()
        rbuf[0] += rbuf[o]

    all_ref[me] = rbuf[0].astype(BF16)

    def g_copy(o):
        peer = lax.rem(chip + o, nc) * 2 + core
        return pltpu.make_async_remote_copy(
            all_ref.at[me], all_ref.at[me], g_sem.at[0, o], g_sem.at[1, o], device_id=dev(peer), device_id_type=pl.DeviceIdType.MESH)

    def f_copy(o):
        src = lax.rem(chip + nc - o, nc) * 2 + core
        return pltpu.make_async_remote_copy(
            all_ref.at[src], all_ref.at[src], f_sem.at[0, o], f_sem.at[1, o], device_id=dev(partner), device_id_type=pl.DeviceIdType.MESH)

    own = pltpu.make_async_remote_copy(
        all_ref.at[me], all_ref.at[me], e_sem.at[0], e_sem.at[1], device_id=dev(partner), device_id_type=pl.DeviceIdType.MESH)

    @pl.loop(1, nc)
    def _(o):
        g_copy(o).start()

    own.start()

    @pl.loop(1, nc)
    def _(o):
        g_copy(o).wait()
        f_copy(o).start()

    own.wait()
    mine.wait()

    @pl.loop(1, nc)
    def _(o):
        f_copy(o).wait()

    @pl.loop(1, n)
    def _(o):
        q_copy(o).wait()


def _tail(dq, dkv, n):
    t, hd = dq.shape
    b = t // n
    nc = n // 2
    vmem = pl.BlockSpec(memory_space=pltpu.VMEM)
    dma = pltpu.SemaphoreType.DMA
    return pl.pallas_call(
        functools.partial(_tail_kernel, n),
        in_specs=[vmem, vmem],
        out_specs=[vmem, vmem],
        out_shape=[jax.ShapeDtypeStruct((n, b, hd), BF16), jax.ShapeDtypeStruct((n, b, 2 * hd), BF16)],
        scratch_shapes=[
            pltpu.VMEM((nc, b, 2 * hd), F32),
            pltpu.VMEM((nc, b, 2 * hd), F32),
            pltpu.VMEM((nc, b, 2 * hd), F32),
            dma((2, n)), dma((2,)), dma((2, nc)), dma((2, nc)), dma((2, nc)), dma((2,)), dma,
        ],
        compiler_params=pltpu.CompilerParams(collective_id=1, has_side_effects=True, vmem_limit_bytes=32 * 2**20),
        cost_estimate=pl.CostEstimate(flops=30 * 10**9, bytes_accessed=16 * t * hd, transcendentals=0),
        name="tail_exchange",
    )(dq.reshape(n, b, hd), dkv.reshape(nc, 2, b, 2 * hd))


def _dx_kernel(nh, dqa_ref, own_ref, wq_ref, wk_ref, wv_ref, dx_ref):
    dims = (((1,), (1,)), ((), ()))

    def term(a0, a1, w0, w1):
        a = jnp.concatenate([a0, a1], axis=1)
        w = jnp.concatenate([w0, w1], axis=1)
        return lax.dot_general(a, w, dims, preferred_element_type=F32)

    hd = wk_ref.shape[1]
    acc = term(own_ref[:, 0:hd], own_ref[:, hd : 2 * hd], wk_ref[...], wv_ref[...])
    for h in range(0, nh, 2):
        acc = acc + term(dqa_ref[h], dqa_ref[h + 1], wq_ref[h], wq_ref[h + 1])
    dx_ref[...] = acc.astype(BF16)


def _dx(dqa, own, wq_all, w_key, w_value):
    nh, b, hd = dqa.shape
    d = w_key.shape[0]
    dt = 512
    return pl.pallas_call(
        functools.partial(_dx_kernel, nh),
        grid=(d // dt,),
        in_specs=[
            pl.BlockSpec((nh, b, hd), lambda i: (0, 0, 0)),
            pl.BlockSpec((b, 2 * hd), lambda i: (0, 0)),
            pl.BlockSpec((nh, dt, hd), lambda i: (0, i, 0)),
            pl.BlockSpec((dt, hd), lambda i: (i, 0)),
            pl.BlockSpec((dt, hd), lambda i: (i, 0)),
        ],
        out_specs=pl.BlockSpec((b, dt), lambda i: (0, i)),
        out_shape=jax.ShapeDtypeStruct((b, d), BF16),
        compiler_params=pltpu.CompilerParams(vmem_limit_bytes=32 * 2**20),
        cost_estimate=pl.CostEstimate(flops=2 * nh * b * d * hd, bytes_accessed=2 * nh * d * hd, transcendentals=0),
        name="dx_rows",
    )(dqa, own, wq_all, w_key, w_value)


def solution(mesh):
    tok_spec = P(("data", "model"), None)
    n = mesh.shape["model"]

    def local_step(x_loc, dy_loc, wq_loc, w_key, w_value, wo_loc):
        d, hd = w_key.shape
        scale = 1.0 / math.sqrt(hd)
        wq_h = wq_loc.reshape(d, hd)
        x_full = lax.all_gather(x_loc, "model", axis=0, tiled=True)
        dy_full = lax.all_gather(dy_loc, "model", axis=0, tiled=True)
        wq_all = lax.all_gather(wq_h, "model", axis=0, tiled=True).reshape(n, d, hd)
        t = x_full.shape[0]
        nb = t // BLK
        w3 = jnp.concatenate([wq_h, w_key, w_value], axis=1)
        qkv = jnp.dot(x_full, w3, preferred_element_type=F32).astype(BF16)
        q, k, v = qkv[:, :hd], qkv[:, hd : 2 * hd], qkv[:, 2 * hd :]
        vt = v.reshape(nb, BLK, hd).transpose(0, 2, 1)
        kt = k.reshape(nb, BLK, hd).transpose(0, 2, 1)
        o, st = _attn_fwd(q, k, vt, scale)
        o, dy_full = lax.optimization_barrier((o, dy_full))
        d_attn = jnp.einsum("td,ed->te", dy_full, wo_loc.reshape(hd, d), preferred_element_type=F32).astype(BF16)
        dq, dkv = _attn_bwd(q, d_attn, o, st, k, v, kt, scale)
        dw_out = jnp.einsum("te,td->ed", o, dy_full, preferred_element_type=F32)[None]
        dw_query = jnp.einsum("td,te->de", x_full, dq, preferred_element_type=F32)[:, None, :]
        dq, dkv, dw_query, dw_out = lax.optimization_barrier((dq, dkv, dw_query, dw_out))
        dqa, dkv_all = _tail(dq, dkv, n)
        me = lax.axis_index("model")
        own = lax.dynamic_index_in_dim(dkv_all, me, 0, keepdims=False)
        dx = _dx(dqa, own, wq_all, w_key, w_value)
        cols = lax.dynamic_slice_in_dim(x_full, me * (d // n), d // n, axis=1)
        dwkv = jnp.einsum("td,te->de", cols, dkv_all.reshape(t, 2 * hd), preferred_element_type=F32)
        return (dx, dw_query, dwkv[:, :hd], dwkv[:, hd:], dw_out)

    return jax.shard_map(
        local_step, mesh=mesh,
        in_specs=(tok_spec, tok_spec, P(None, "model", None), P(None, None), P(None, None), P("model", None, None)),
        out_specs=(tok_spec, P("data", "model", None), tok_spec, tok_spec, P(("data", "model"), None, None)),
        check_vma=False)
```

time: 932 us -> 429 us (0.46)
  waiting for transfers between devices: 621 us -> 169 us
  matrix products: 255 us -> 70.8 us
  Pallas kernels: 0 us -> 156 us
  other arithmetic: 21.7 us -> 0 us
    reduce_scatter x5 -> x0, waiting for transfers between devices: 424 us -> none  [the longest x1 288 us: local_step(): dx_sum = lax.psum_scatter(dx_part, 'model', scatter_dimension=0, tiled=True)]
    dot_general x17 -> x5, matrix products: 255 us -> 70.8 us  [the longest x1 23.1 us: local_step(): qkv = jnp.dot(x_full, w3, preferred_element_type=F32).astype(BF16)]
    pallas_call x0 -> x4, Pallas kernels: none -> 156 us  [the longest x1 79.8 us: _tail(): pl.pallas_call(functools.partial(_tail_kernel, n), in_specs=[vmem, vmem],...]
    all_gather x2 -> x1, waiting for transfers between devices: 24.1 us -> 0.01 us  [local_step(): wq_all = lax.all_gather(wq_h, 'model', axis=0, tiled=True).reshape(n, d, hd)]
    reduce_sum x1 -> x0, other arithmetic: 21.7 us -> none  [local_step(): probs_f32 = jax.nn.softmax(scores, axis=-1)]
    all_gather x1, waiting for transfers between devices: 63.2 us -> 53.9 us  [local_step(): dy_full = lax.all_gather(dy_loc, 'model', axis=0, tiled=True)]
  transfers between devices with their start and end apart: 9 -> 3, of which waited for: 6 -> 2; matrix products, arithmetic and copies ran while one was open for 31% -> 19% of each run, Pallas kernels for 0% -> 32%
where the time goes in v1:
time: 429 us; the launch traced here: 428 us
  waiting for transfers between devices  169 us (39%)
  Pallas kernels  156 us (36%)
  matrix products  70.8 us (17%)
  local copies, waits for them, and re-layouts  18.6 us (4%)
  between operations  13.9 us (3%)
    all_gather x1, waiting for transfers between devices, local_step(): x_full = lax.all_gather(x_loc, 'model', axis=0, tiled=True)  113 us
    pallas_call x1, Pallas kernels, _tail(): pl.pallas_call(functools.partial(_tail_kernel, n), in_specs=[vmem, vmem],...  79.8 us
    all_gather x1, waiting for transfers between devices, local_step(): dy_full = lax.all_gather(dy_loc, 'model', axis=0, tiled=True)  53.9 us
    pallas_call x1, Pallas kernels, _attn_bwd(): pl.pallas_call(functools.partial(_bwd_kernel, scale), grid=(n,), in_specs...  31.5 us
    pallas_call x1, Pallas kernels, _attn_fwd(): pl.pallas_call(functools.partial(_fwd_kernel, scale), grid=(n,), in_specs...  26.4 us
    dot_general x1, matrix products, local_step(): qkv = jnp.dot(x_full, w3, preferred_element_type=F32).astype(BF16)  23.1 us
    pallas_call x1, Pallas kernels, _dx(): pl.pallas_call(functools.partial(_dx_kernel, nh), grid=(d // dt,), in_spe...  18 us
    dot_general x1, matrix products, local_step(): jnp.einsum('te,td->ed', o, dy_full, preferred_element_type=F32)[None]  16.7 us
  transfers between devices with their start and end apart: 3, of which 2 were waited for; matrix products, arithmetic and copies ran while one was open for 19% of the time, Pallas kernels for 32%

profile of v1, /device:TPU:97, one launch (start us, length us, event | category | flops | bytes accessed | tf_op | source)
XLA Modules:
  0.0 428.1 jit_solution(10804855900810057562)
XLA Ops:
  7.2 0.0 copy-start
  7.2 0.1 all-gather.5.cloned.1.call-start
  7.3 0.7 all-gather.5.cloned.1.call-update
  8.0 0.1 all-gather.7.cloned.1.call-start
  8.1 0.7 all-gather.7.cloned.1.call-update
  8.8 0.1 all-gather.9.cloned.1.call-start
  8.9 0.7 all-gather.9.cloned.1.call-update
  9.6 113.0 %all-gather.5.cloned.1.call-done = bf16[4096,4096]{1,0:T(8,128)(2,1)} async-done(((bf16[128,4096]{1,0:T(8,128)(2,1)}), bf16[4096,4096]{1,0:T(8,128)(2,1)}) %all-gather.5.cloned.1.call-update) | async-done | bytes 33554448 | tf_op jit(solution)/shard_map/all_gather | solution.py:296
  122.6 23.1 %fusion = bf16[4096,384]{1,0:T(8,128)(2,1)S(1)} fusion(bf16[4096,4096]{1,0:T(8,128)(2,1)} %all-gather.5.cloned.1.call-done, bf16[4096,128]{1,0:T(8,128)(2,1)} %wv_ref.1, bf16[4096,128]{1,0:T(8,128)(2,1)} %wk_ref.1, bf16[4096,128]{1,0:T(8,128)(2,1)} %bitcast.37), kind=kOutput, calls=%fused_computation.1 | convolution fusion | flops 12895911936 | bytes 39845888 | tf_op jit(solution)/shard_map/dot_general | solution.py:302
  145.8 1.5 fusion.11
  147.3 1.3 copy.15
  148.6 0.0 copy-start.11
  148.6 1.2 copy-done.11
  149.8 0.0 copy-start.12
  149.8 1.2 copy-done.12
  151.0 26.4 %attn_fwd.1 = (bf16[4096,128]{1,0:T(8,128)(2,1)S(1)}, f32[8,4096]{1,0:T(8,128)S(1)}) custom-call(bf16[4096,128]{1,0:T(8,128)(2,1)S(1)} %copy-done.12, bf16[4096,128]{1,0:T(8,128)(2,1)S(1)} %get-tuple-element.40.k_ref, bf16[8,128,512]{2,1,0:T(8,128)(2,1)S(1)} %bitcast.34), custom_call_target="tpu_custom_call" | custom-call | flops 40000000000 | bytes 4194304 | tf_op jit(solution)/shard_map/attn_fwd/pallas_call | solution.py:96
  177.4 0.0 copy-start.2
  177.4 1.0 copy-done.2
  178.4 53.9 %all-gather.7.cloned.1.call-done = bf16[4096,4096]{1,0:T(8,128)(2,1)} async-done(((bf16[128,4096]{1,0:T(8,128)(2,1)}), bf16[4096,4096]{1,0:T(8,128)(2,1)}) %all-gather.7.cloned.1.call-update) | async-done | bytes 33554448 | tf_op jit(solution)/shard_map/all_gather | solution.py:297
  232.2 1.3 copy.16
  233.5 16.7 %convolution_bitcast_fusion = f32[1,128,4096]{2,1,0:T(8,128)} fusion(bf16[4096,128]{1,0:T(8,128)(2,1)} %copy-done.2, bf16[4096,4096]{1,0:T(8,128)(2,1)} %all-gather.7.cloned.1.call-done), kind=kOutput, calls=%fused_computation.2 | convolution fusion | flops 4294967296 | bytes 36700160 | tf_op jit(solution)/shard_map/te,td->ed/dot_general | solution.py:310
  250.3 0.0 copy-done
  250.3 0.0 copy-start.3
  250.3 0.0 copy-start.10
  250.3 0.0 copy-start.13
  250.3 15.5 %convolution_convert_fusion.1.do_ref = bf16[4096,128]{1,0:T(8,128)(2,1)S(1)} fusion(bf16[4096,4096]{1,0:T(8,128)(2,1)} %all-gather.7.cloned.1.call-done, bf16[1,128,4096]{2,1,0:T(8,128)(2,1)S(1)} %copy-done), kind=kOutput, calls=%fused_computation.4 | convolution fusion | flops 4295491584 | bytes 35651584 | tf_op jit(solution)/shard_map/td,ed->te/dot_general | solution.py:308
  265.8 0.0 copy-done.3
  265.8 0.0 copy-done.10
  265.8 0.0 copy-done.13
  265.8 31.5 %attn_bwd.1 = (bf16[4096,128]{1,0:T(8,128)(2,1)S(1)}, f32[4096,256]{1,0:T(8,128)S(1)}) custom-call(bf16[4096,128]{1,0:T(8,128)(2,1)S(1)} %copy-done.13, bf16[4096,128]{1,0:T(8,128)(2,1)S(1)} %convolution_convert_fusion.1.do_ref, bf16[4096,128]{1,0:T(8,128)(2,1)S(1)} %copy-done.3, f32[8,4096]{1,0:T(8,128)S(1)} %get-tuple-element.20.st_ref, ...), custom_call_target="tpu_custom_call" | custom-call | flops 60000002048 | bytes 8388608 | tf_op jit(solution)/shard_map/attn_bwd/pallas_call | solution.py:118
  297.3 0.0 copy-start.14
  297.3 2.0 copy-done.14
  299.3 0.0 copy-start.4
  299.3 13.3 %convolution_bitcast_fusion.1 = f32[4096,1,128]{0,2,1:T(8,128)S(1)} fusion(bf16[4096,128]{1,0:T(8,128)(2,1)S(1)} %get-tuple-element.23, bf16[4096,4096]{1,0:T(8,128)(2,1)} %all-gather.5.cloned.1.call-done), kind=kOutput, calls=%fused_computation.3 | convolution fusion | flops 4294967296 | bytes 36700160 | tf_op jit(solution)/shard_map/td,te->de/dot_general | solution.py:311
  312.6 0.0 copy-done.4
  312.6 3.7 copy.17
  316.3 1.2 copy-done.5
  317.5 2.2 copy-done.15
  319.7 79.8 %tail_exchange.1 = (bf16[32,128,128]{2,1,0:T(8,128)(2,1)S(1)}, bf16[32,128,256]{2,1,0:T(8,128)(2,1)S(1)}) custom-call(bf16[32,128,128]{2,1,0:T(8,128)(2,1)S(1)} %bitcast.32, f32[16,2,128,256]{3,2,1,0:T(8,128)S(1)} %bitcast.35), custom_call_target="tpu_custom_call" | custom-call | flops 30000001024 | bytes 8388608 | tf_op jit(solution)/shard_map/tail_exchange/pallas_call | solution.py:234
  399.5 0.0 copy-start.8
  399.6 2.1 fusion.7
  401.7 0.0 copy-done.8
  401.7 0.7 fusion.12
  402.4 0.0 copy-done.6
  402.4 0.0 copy-done.7
  402.4 1.2 copy-done.9
  403.6 18.0 %dx_rows.1 = bf16[128,4096]{1,0:T(8,128)(2,1)} custom-call(bf16[32,128,128]{2,1,0:T(8,128)(2,1)S(1)} %copy-done.9, bf16[128,256]{1,0:T(8,128)(2,1)S(1)} %dynamic-slice_bitcast_fusion.own_ref, bf16[32,4096,128]{2,1,0:T(8,128)(2,1)} %bitcast.36, bf16[4096,128]{1,0:T(8,128)(2,1)S(1)} %copy-done.7, bf16[4096,128]{1,0:T(8,128)(2,1)S(1)} %copy-done.6), custom_call_target="tpu_custom_call" | custom-call | flops 4294967296 | bytes 33554432 | tf_op jit(solution)/shard_map/dx_rows/pallas_call | solution.py:270
  421.6 0.0 copy-done.1
  (8 shorter events, 0.0 us)
Async XLA Ops:
  7.2 243.1 %copy-start = (bf16[1,128,4096]{2,1,0:T(8,128)(2,1)S(1)}, bf16[1,128,4096]{2,1,0:T(8,128)(2,1)}, u32[]{:S(2)}) copy-start(bf16[1,128,4096]{2,1,0:T(8,128)(2,1)} %param.11) | copy-start | bytes 3145732
  7.2 115.4 %all-gather.5.cloned.1.call-start = ((), (), s32[]{:S(2)}) async-start(), calls=%async_computation | async-start | bytes 34603008 | tf_op jit(solution)/shard_map/all_gather | solution.py:296
  8.0 224.2 %all-gather.7.cloned.1.call-start = ((), (), s32[]{:S(2)}) async-start(), calls=%async_computation.1 | async-start | bytes 34603008 | tf_op jit(solution)/shard_map/all_gather | solution.py:297
  8.8 393.6 %all-gather.9.cloned.1.call-start = ((), (), s32[]{:S(2)}) async-start(), calls=%async_computation.2 | async-start | bytes 34603008 | tf_op jit(solution)/shard_map/all_gather | solution.py:298
  148.6 1.2 copy-start.11
  149.8 1.2 copy-start.12
  177.4 1.0 copy-start.2
  250.3 15.6 %copy-start.3 = (bf16[4096,128]{1,0:T(8,128)(2,1)S(1)}, bf16[4096,128]{1,0:T(8,128)(2,1)}, u32[]{:S(2)}) copy-start(bf16[4096,128]{1,0:T(8,128)(2,1)} %copy-done.2) | copy-start | bytes 3145732
  250.3 15.6 %copy-start.10 = (bf16[8,512,128]{1,2,0:T(8,128)(2,1)S(1)}, bf16[8,512,128]{1,2,0:T(8,128)(2,1)}, u32[]{:S(2)}) copy-start(bf16[8,512,128]{1,2,0:T(8,128)(2,1)} %copy.16) | copy-start | bytes 3145732
  250.3 15.6 %copy-start.13 = (bf16[4096,128]{1,0:T(8,128)(2,1)S(1)}, bf16[4096,128]{1,0:T(8,128)(2,1)}, u32[]{:S(2)}) copy-start(bf16[4096,128]{1,0:T(8,128)(2,1)} %get-tuple-element.41.q_ref) | copy-start | bytes 3145732
  297.3 2.0 copy-start.14
  299.3 13.3 %copy-start.4 = (bf16[4096,128]{1,0:T(8,128)(2,1)}, bf16[4096,128]{1,0:T(8,128)(2,1)S(1)}, u32[]{:S(2)}) copy-start(bf16[4096,128]{1,0:T(8,128)(2,1)S(1)} %get-tuple-element.23) | copy-start | bytes 3145732
  316.3 1.2 copy-start.5
  317.5 2.2 copy-start.15
  319.7 82.6 %copy-start.6 = (bf16[4096,128]{1,0:T(8,128)(2,1)S(1)}, bf16[4096,128]{1,0:T(8,128)(2,1)}, u32[]{:S(2)}) copy-start(bf16[4096,128]{1,0:T(8,128)(2,1)} %wv_ref.1) | copy-start | bytes 3145732
  319.7 82.6 %copy-start.7 = (bf16[4096,128]{1,0:T(8,128)(2,1)S(1)}, bf16[4096,128]{1,0:T(8,128)(2,1)}, u32[]{:S(2)}) copy-start(bf16[4096,128]{1,0:T(8,128)(2,1)} %wk_ref.1) | copy-start | bytes 3145732
  399.5 2.2 copy-start.8
  402.4 1.2 copy-start.9
  403.6 18.0 %copy-start.1 = (bf16[1,128,4096]{2,1,0:T(8,128)(2,1)S(1)}, bf16[1,128,4096]{2,1,0:T(8,128)(2,1)}, u32[]{:S(2)}) copy-start(bf16[1,128,4096]{2,1,0:T(8,128)(2,1)} %param.11) | copy-start | bytes 3145732
Sparse Core Ops, SparseCore 0:
  10.1 112.4 all-gather.4
  124.7 107.4 all-gather.6
  234.3 139.4 all-gather.8

commit v2 on v0

v2 whole, which is shorter than its diff:
```python
import functools
import math
import jax
import jax.numpy as jnp
from jax import lax
from jax.experimental import pallas as pl
from jax.experimental.pallas import tpu as pltpu
from jax.sharding import PartitionSpec as P

BLK = 512
F32 = jnp.float32
BF16 = jnp.bfloat16
MESH_ID = pl.DeviceIdType.MESH


def _dot(a, b):
    return jnp.dot(a, b, preferred_element_type=F32)


def _flip(a):
    return jnp.transpose(a.astype(F32))


def _fwd_block(scale, i, q_ref, k_ref, vt_ref, ot_ref, st_ref, s_ref):
    here = pl.ds(pl.multiple_of(i * BLK, BLK), BLK)
    qt = _flip(q_ref[here, :]).astype(BF16)

    def score(j, m8, diag):
        s = _dot(k_ref[pl.ds(pl.multiple_of(j * BLK, BLK), BLK), :], qt) * scale
        if diag:
            key = lax.broadcasted_iota(jnp.int32, (BLK, BLK), 0)
            qry = lax.broadcasted_iota(jnp.int32, (BLK, BLK), 1)
            s = jnp.where(qry >= key, s, -jnp.inf)
        s_ref[j] = s
        return jnp.maximum(m8, jnp.max(s.reshape(BLK // 8, 8, BLK), axis=0))

    m8 = jnp.full((8, BLK), -jnp.inf, F32)
    m8 = lax.fori_loop(0, i, lambda j, c: score(j, c, False), m8)
    m8 = score(i, m8, True)
    m = jnp.max(m8, axis=0, keepdims=True)

    def expo(j, l8):
        p = jnp.exp(s_ref[j] - m)
        s_ref[j] = p
        return l8 + jnp.sum(p.reshape(BLK // 8, 8, BLK), axis=0)

    l8 = lax.fori_loop(0, i + 1, expo, jnp.zeros((8, BLK), F32))
    r = 1.0 / jnp.sum(l8, axis=0, keepdims=True)

    def attend(j, ot):
        return ot + _dot(vt_ref[j], (s_ref[j] * r).astype(BF16))

    ot = lax.fori_loop(0, i + 1, attend, jnp.zeros(ot_ref.shape[1:], F32))
    ot_ref[i] = ot.astype(BF16)
    row = lax.broadcasted_iota(jnp.int32, (8, BLK), 0)
    st_ref[i] = jnp.where(row == 0, m, r)


def _bwd_block(scale, i, q_ref, do_ref, ot_ref, st_ref, k_ref, v_ref, kt_ref, dq_ref, dqt_ref, dkv_ref):
    here = pl.ds(pl.multiple_of(i * BLK, BLK), BLK)
    hd = q_ref.shape[1]
    qt = _flip(q_ref[here, :]).astype(BF16)
    dot_f = _flip(do_ref[here, :])
    c = jnp.sum(dot_f * ot_ref[i].astype(F32), axis=0, keepdims=True)
    dot_b = dot_f.astype(BF16)
    m = st_ref[i, 0:1, :]
    r = st_ref[i, 1:2, :]
    chips = BLK // (dkv_ref.shape[1] * dkv_ref.shape[2])

    def step(j, dqt, diag):
        rows = pl.ds(pl.multiple_of(j * BLK, BLK), BLK)
        s = _dot(k_ref[rows, :], qt) * scale
        if diag:
            key = lax.broadcasted_iota(jnp.int32, (BLK, BLK), 0)
            qry = lax.broadcasted_iota(jnp.int32, (BLK, BLK), 1)
            s = jnp.where(qry >= key, s, -jnp.inf)
        p = jnp.exp(s - m) * r
        dp = _dot(v_ref[rows, :], dot_b)
        g = (p * (dp - c) * scale).astype(BF16)
        dk = _dot(g, q_ref[here, :])
        dv = _dot(p.astype(BF16), do_ref[here, :])
        at = pl.ds(j * chips, chips)
        shape = (chips, *dkv_ref.shape[1:3], hd)
        dkv_ref[at, :, :, 0:hd] += dk.reshape(shape)
        dkv_ref[at, :, :, hd : 2 * hd] += dv.reshape(shape)
        return dqt + _dot(kt_ref[j], g)

    dqt = jnp.zeros((hd, BLK), F32)
    dqt = lax.fori_loop(0, i, lambda j, a: step(j, a, False), dqt)
    dqt = step(i, dqt, True)
    dqt_ref[i] = dqt.astype(BF16)
    dq_ref[pl.ds(i * chips, chips)] = jnp.transpose(dqt).astype(BF16).reshape(chips, *dq_ref.shape[1:])


def _torus_messages():
    msgs = {}
    for s in (1, -1):
        msgs["S1", 0, s] = len(msgs)
    for s in (1, -1):
        msgs["F1", 0, s] = len(msgs)
    for a in (0, -1, 1, 2):
        for s in (1, -1):
            msgs["S2", a, s] = len(msgs)
    for a in (0, -1, 1, 2):
        for s in (1, -1):
            msgs["F2", a, s] = len(msgs)
    return msgs


class _TorusGather:
    def __init__(self, n, x_ref, out_ref, l_sem, i_sem, d_sem=None, o_sem=None):
        self.me = me = lax.axis_index("model")
        self.core = lax.rem(me, 2)
        chip = me // 2
        self.side = math.isqrt(n // 2)
        assert self.side == 4
        self.cx, self.cy = lax.rem(chip, self.side), chip // self.side
        self.partner = me + 1 - 2 * self.core
        self.x_ref, self.out_ref, self.i_sem, self.d_sem = x_ref, out_ref, i_sem, d_sem
        self.msgs = _torus_messages()
        self.sent, self.handed, self.handed_in = [], [], []
        self.own = o_sem is not None and pltpu.make_async_remote_copy(
            x_ref, out_ref.at[me], o_sem.at[0], o_sem.at[1], device_id={"model": self.partner}, device_id_type=MESH_ID)
        self.mine = pltpu.make_async_copy(x_ref, out_ref.at[me], l_sem)

    def chip_at(self, dx, dy):
        side = self.side
        return lax.rem(self.cy + dy + side, side) * side + lax.rem(self.cx + dx + side, side)

    def device(self, part, a, b):
        dx, dy = (a, b) if part == 0 else (b, a)
        return self.chip_at(dx, dy) * 2 + self.core

    def region(self, ref, part, hs):
        return ref.at[pl.ds(2 * part + (hs < 0), 2 if hs == 0 else 1)]

    def number(self, m):
        return m[0] * len(self.msgs) + self.msgs[m[1:]]

    def message(self, m):
        part, kind, a, s = m
        i = self.number(m)
        if kind in ("S1", "F1"):
            to = self.device(part, s, 0)
            src = (0, 0) if kind == "S1" else (-s, 0)
        else:
            to = self.device(part, 0, s)
            src = (a, 0) if kind == "S2" else (a, -s)
        hs = s if kind in ("F1", "F2") else 0
        dst = self.out_ref.at[self.device(part, *src)]
        frm = self.x_ref if src == (0, 0) else dst
        return pltpu.make_async_remote_copy(
            self.region(frm, part, hs), self.region(dst, part, hs), self.i_sem.at[0, i], self.i_sem.at[1, i],
            device_id={"model": to}, device_id_type=MESH_ID)

    def piece(self, m, sem):
        part, kind, a, s = m
        i = self.number(m)
        off = {"S1": (-s, 0), "F1": (2, 0), "S2": (a, -s), "F2": (a, 2)}[kind]
        ref = self.region(self.out_ref.at[self.device(part, *off)], part, s if kind in ("F1", "F2") else 0)
        return pltpu.make_async_remote_copy(
            ref, ref, sem.at[0, i], sem.at[1, i], device_id={"model": self.partner}, device_id_type=MESH_ID)

    def send(self, *m):
        self.message(m).start()
        self.sent.append(m)

    def got(self, *m):
        self.piece(m, self.i_sem).wait_recv()
        if self.d_sem is not None:
            self.piece(m, self.d_sem).start()
            self.handed.append(m)

    def start(self):
        for kind in ("S1", "S2"):
            for part in (0, 1):
                for s in (1, -1):
                    self.send(part, kind, 0, s)
        if self.own:
            self.own.start()
        self.mine.start()

    def first(self):
        for s in (1, -1):
            for part in (0, 1):
                self.got(part, "S1", 0, s)
                self.send(part, "F1", 0, s)
                for z in (1, -1):
                    self.send(part, "S2", -s, z)

    def second(self):
        for part in (0, 1):
            for s in (1, -1):
                self.got(part, "F1", 0, s)
            for z in (1, -1):
                self.send(part, "S2", 2, z)

    def third(self, k):
        a, s = (0, -1, 1, 2)[k // 2], (1, -1)[k % 2]
        for part in (0, 1):
            self.got(part, "S2", a, s)
            self.send(part, "F2", a, s)

    def last(self, k):
        a = (0, -1, 1, 2)[k]
        for s in (1, -1):
            for part in (0, 1):
                self.got(part, "F2", a, s)
                if self.d_sem is not None:
                    self.handed_in.append((part, "F2", a, s))
        for m in self.handed_in:
            self.piece(m, self.d_sem).wait_recv()
        self.handed_in = []

    def inner_ready(self):
        self.mine.wait()
        if self.own:
            self.own.wait_recv()
            for part in (0, 1):
                for m in self.msgs:
                    if m[0] != "F2":
                        self.piece((part, *m), self.d_sem).wait_recv()

    def finish(self):
        for m in self.sent:
            self.message(m).wait_send()
        for m in self.handed:
            self.piece(m, self.d_sem).wait_send()
        if self.own:
            self.own.wait_send()


def _step_kernel(n, scale, x_ref, dy_ref, wq_ref, wk_ref, wv_ref, wo_ref,
                 xf_ref, dyf_ref, wqf_ref, dx_ref, dwq_ref, dwk_ref, dwv_ref, dwo_ref,
                 w3_ref, q_ref, k_ref, v_ref, kt_ref, vt_ref, ot_ref, st_ref, do_ref, dq_ref, dqt_ref, s_ref, buf, wbuf,
                 dkv_ref, pbuf, rbuf, all_ref, dqa_ref, xc_ref,
                 xl, xi, xd, xo, yl, yi, yd, yo, wl, wi, b_sem, c_sem, p_sem, q_sem, r_sem, g_sem, f_sem, e_sem, a_sem):
    gx = _TorusGather(n, x_ref, xf_ref, xl, xi, xd, xo)
    gy = _TorusGather(n, dy_ref, dyf_ref, yl, yi, yd, yo)
    gw = _TorusGather(n, wq_ref, wqf_ref, wl, wi)
    me, core, partner = gx.me, gx.core, gx.partner
    chip = me // 2
    nc = n // 2
    d, hd = wk_ref.shape
    nb = st_ref.shape[0]
    per = x_ref.shape[0] * x_ref.shape[1]
    rows = 2 * per

    def dev(idx):
        return {"model": idx}

    def remote(src, dst, sem, to):
        return pltpu.make_async_remote_copy(src, dst, sem[0], sem[1], device_id=dev(to), device_id_type=MESH_ID)

    def peer(o):
        return lax.rem(chip + o, nc) * 2 + core

    barrier = pltpu.get_barrier_semaphore()

    @pl.loop(1, nc)
    def _(o):
        pl.semaphore_signal(barrier, inc=1, device_id=dev(peer(o)), device_id_type=MESH_ID)

    pl.semaphore_signal(barrier, inc=1, device_id=dev(partner), device_id_type=MESH_ID)
    pl.semaphore_wait(barrier, nc)

    gx.start()

    def near(k):
        return gx.chip_at(lax.rem(k, 3) - 1, k // 3 - 1)

    def far(k):
        g = k // 2
        v = jnp.where(g == 3, 2, jnp.where(g == 2, 1, -g))
        even = lax.rem(k, 2) == 0
        return gx.chip_at(jnp.where(even, 2, v), jnp.where(even, v, 2))

    def rows_of(c):
        return pl.ds(pl.multiple_of(c * rows, rows), rows)

    def over_near(src_ref, work):
        def load(k):
            slot = lax.rem(k, 2)
            return pltpu.make_async_copy(src_ref.at[pl.ds(2 * near(k), 2)], buf.at[slot, pl.ds(0, 2)], b_sem.at[slot])

        load(0).start()

        @pl.loop(0, 9)
        def _(k):
            load(k).wait()

            @pl.when(k + 1 < 9)
            def _():
                load(k + 1).start()

            work(buf[lax.rem(k, 2), 0:2].reshape(rows, d), rows_of(near(k)))

    def over_far(g, src_ref, work):
        @pl.loop(0, 7)
        def _(k):
            for z in range(4):
                @pl.when(k == 2 * z)
                def _():
                    g.last(z)

            load = pltpu.make_async_copy(src_ref.at[pl.ds(2 * far(k), 2)], buf.at[0, pl.ds(0, 2)], b_sem.at[0])
            load.start()
            load.wait()
            work(buf[0, 0:2].reshape(rows, d), rows_of(far(k)))

    def project(block, here):
        r = _dot(block, w3_ref[...]).astype(BF16)
        q_ref[here, :] = r[:, :hd]
        k_ref[here, :] = r[:, hd : 2 * hd]
        v_ref[here, :] = r[:, 2 * hd :]

    def project_dy(block, here):
        do_ref[here, :] = lax.dot_general(
            block, wo_ref[...], (((1,), (1,)), ((), ())), preferred_element_type=F32).astype(BF16)

    w3_ref[:, 0:hd] = wq_ref[...].reshape(d, hd)
    w3_ref[:, hd : 2 * hd] = wk_ref[...]
    w3_ref[:, 2 * hd :] = wv_ref[...]
    dkv_ref[...] = jnp.zeros_like(dkv_ref)

    gx.first()
    gx.second()
    for k in range(8):
        gx.third(k)
    gy.start()
    gx.inner_ready()
    over_near(xf_ref, project)
    gy.first()
    over_far(gx, xf_ref, project)
    gy.second()
    cols = pltpu.make_async_copy(
        xf_ref.at[:, :, :, pl.ds(pl.multiple_of(me * (d // n), d // n), d // n)], xc_ref, c_sem)
    cols.start()

    @pl.loop(0, nb)
    def _(j):
        here = pl.ds(pl.multiple_of(j * BLK, BLK), BLK)
        vt_ref[j] = _flip(v_ref[here, :]).astype(BF16)
        kt_ref[j] = _flip(k_ref[here, :]).astype(BF16)

    @pl.loop(0, nb)
    def _(i):
        for k in range(8):
            @pl.when(i == k)
            def _():
                gy.third(k)

        _fwd_block(scale, i, q_ref, k_ref, vt_ref, ot_ref, st_ref, s_ref)

    gw.start()
    gy.inner_ready()
    over_near(dyf_ref, project_dy)
    over_far(gy, dyf_ref, project_dy)

    @pl.loop(0, nb)
    def _(i):
        @pl.when(i == 4)
        def _():
            gw.first()

        @pl.when(i == 6)
        def _():
            gw.second()

        _bwd_block(scale, i, q_ref, do_ref, ot_ref, st_ref, k_ref, v_ref, kt_ref, dq_ref, dqt_ref, dkv_ref)

    pair = remote(dkv_ref.at[:, 1 - core], pbuf, (p_sem.at[0], p_sem.at[1]), partner)
    pair.start()

    def q_copy(o):
        return remote(dq_ref.at[lax.rem(chip + o, nc)], dqa_ref.at[chip], (q_sem.at[0, o], q_sem.at[1, o]), peer(o))

    @pl.loop(1, nc)
    def _(o):
        q_copy(o).start()

    dqa_ref[chip] = dq_ref[chip]
    gw.third(0)
    gw.third(1)
    pair.wait()

    def r_copy(o):
        return remote(pbuf.at[lax.rem(chip + o, nc)], rbuf.at[o], (r_sem.at[0, o], r_sem.at[1, o]), peer(o))

    @pl.loop(1, nc)
    def _(o):
        t = lax.rem(chip + o, nc)
        pbuf[t] += dkv_ref[t, core]
        r_copy(o).start()

    rbuf[0] = pbuf[chip] + dkv_ref[chip, core]

    def over_blocks(src_ref, work, pump):
        def load(j):
            slot = lax.rem(j, 2)
            return pltpu.make_async_copy(src_ref.at[pl.ds(4 * j, 4)], buf.at[slot], b_sem.at[slot])

        load(0).start()

        @pl.loop(0, nb)
        def _(j):
            load(j).wait()

            @pl.when(j + 1 < nb)
            def _():
                load(j + 1).start()

            for at, ks in pump.items():
                @pl.when(j == at)
                def _():
                    for k in ks:
                        gw.third(k)

            @pl.loop(0, nb)
            def _(c):
                work(j, c, buf[lax.rem(j, 2), :, :, :, pl.ds(pl.multiple_of(c * BLK, BLK), BLK)].reshape(BLK, BLK))

    def out_grad(j, c, block):
        here = pl.ds(pl.multiple_of(c * BLK, BLK), BLK)
        r = _dot(ot_ref[j], block)
        dwo_ref[:, here] = jnp.where(j == 0, r, dwo_ref[:, here] + r)

    def query_grad(j, c, block):
        r = _dot(dqt_ref[j], block)
        s_ref[c, 3 * hd : 4 * hd] = jnp.where(j == 0, r, s_ref[c, 3 * hd : 4 * hd] + r)

    dwo_ref[...] = jnp.zeros_like(dwo_ref)
    s_ref[:, 3 * hd : 4 * hd] = jnp.zeros((nb, hd, BLK), F32)
    over_blocks(dyf_ref, out_grad, {0: (2, 3), 4: (4, 5), 7: (6, 7)})

    @pl.loop(1, nc)
    def _(o):
        r_copy(o).wait()
        rbuf[0] += rbuf[o]

    all_ref[me] = rbuf[0].astype(BF16)

    def g_copy(o):
        return remote(all_ref.at[me], all_ref.at[me], (g_sem.at[0, o], g_sem.at[1, o]), peer(o))

    def f_copy(o):
        src = lax.rem(chip + nc - o, nc) * 2 + core
        return remote(all_ref.at[src], all_ref.at[src], (f_sem.at[0, o], f_sem.at[1, o]), partner)

    own = remote(all_ref.at[me], all_ref.at[me], (e_sem.at[0], e_sem.at[1]), partner)

    @pl.loop(1, nc)
    def _(o):
        g_copy(o).start()

    own.start()
    over_blocks(xf_ref, query_grad, {})

    @pl.loop(0, nb)
    def _(c):
        dwq_ref[pl.ds(pl.multiple_of(c * BLK, BLK), BLK), :] = jnp.transpose(s_ref[c, 3 * hd : 4 * hd])

    @pl.loop(1, nc)
    def _(o):
        q_copy(o).wait()

    gw.inner_ready()
    both = (((1,), (1,)), ((), ()))

    def chip_of(k):
        return jnp.where(k < 9, near(k), far(k - 9))

    def add_heads(z):
        c0, c1 = chip_of(2 * z), chip_of(2 * z + 1)
        a = jnp.concatenate([dqa_ref[c0], dqa_ref[c1]], axis=1)

        @pl.loop(0, nb)
        def _(c):
            here = pl.ds(pl.multiple_of(c * BLK, BLK), BLK)
            w = jnp.concatenate([wbuf[0, here, :], wbuf[1, here, :]], axis=1)
            r = lax.dot_general(a, w, both, preferred_element_type=F32)
            s_ref[c, 0:rows] = jnp.where(z == 0, r, s_ref[c, 0:rows] + r)

    s_ref[:, 0:rows] = jnp.zeros((nb, rows, BLK), F32)

    @pl.loop(0, 8)
    def _(z):
        for f in range(4):
            @pl.when(z == 4 + f)
            def _():
                gw.last(f)

        for u in (0, 1):
            pltpu.make_async_copy(
                wqf_ref.at[2 * chip_of(2 * z + u) + core], wbuf.at[u].reshape(wq_ref.shape), b_sem.at[u]).start()
        for u in (0, 1):
            pltpu.make_async_copy(
                wqf_ref.at[2 * chip_of(2 * z + u) + core], wbuf.at[u].reshape(wq_ref.shape), b_sem.at[u]).wait()
        add_heads(z)

    swap = remote(s_ref.at[:, pl.ds(pl.multiple_of((1 - core) * per, per), per)], s_ref.at[:, pl.ds(rows, per)],
                  (a_sem.at[0], a_sem.at[1]), partner)
    swap.start()

    @pl.loop(1, nc)
    def _(o):
        g_copy(o).wait()
        f_copy(o).start()

    own.wait()
    cols.wait()

    @pl.loop(1, nc)
    def _(o):
        f_copy(o).wait()

    def key_grad(j, acc):
        xt = _flip(xc_ref[pl.ds(4 * j, 4)].reshape(BLK, d // n)).astype(BF16)
        return acc + _dot(xt, all_ref[pl.ds(4 * j, 4)].reshape(BLK, 2 * hd))

    r = lax.fori_loop(0, nb, key_grad, jnp.zeros((d // n, 2 * hd), F32))
    dwk_ref[...] = r[:, :hd]
    dwv_ref[...] = r[:, hd:]
    swap.wait()
    mine = all_ref[me]

    @pl.loop(0, nb)
    def _(c):
        here = pl.ds(pl.multiple_of(c * BLK, BLK), BLK)
        w = jnp.concatenate([wk_ref[here, :], wv_ref[here, :]], axis=1)
        r = lax.dot_general(mine, w, both, preferred_element_type=F32)
        at = pl.ds(pl.multiple_of(core * per, per), per)
        dx_ref[:, here] = (s_ref[c, at] + s_ref[c, rows : rows + per] + r).astype(BF16)

    gx.finish()
    gy.finish()
    gw.finish()


def _step(x, dy, wq, wk, wv, wo, n, scale):
    rows, d = x.shape
    hd = wo.shape[0]
    t = n * rows
    nb = t // BLK
    nc = n // 2
    assert nb == 8 and 4 * rows == BLK
    nm = 2 * len(_torus_messages())
    hbm = pl.BlockSpec(memory_space=pltpu.HBM)
    vmem = pl.BlockSpec(memory_space=pltpu.VMEM)
    dma = pltpu.SemaphoreType.DMA
    full = jax.ShapeDtypeStruct((n, 4, rows // 4, d), BF16)
    head = pltpu.VMEM((t, hd), BF16)
    flat = pltpu.VMEM((nb, hd, BLK), BF16)
    return pl.pallas_call(
        functools.partial(_step_kernel, n, scale),
        in_specs=[hbm, hbm] + [vmem] * 4,
        out_specs=[hbm] * 3 + [vmem] * 5,
        out_shape=[
            full, full, jax.ShapeDtypeStruct((n, 4, d // 4, hd), BF16),
            jax.ShapeDtypeStruct((rows, d), BF16), jax.ShapeDtypeStruct((d, hd), F32),
            jax.ShapeDtypeStruct((d // n, hd), F32), jax.ShapeDtypeStruct((d // n, hd), F32),
            jax.ShapeDtypeStruct((hd, d), F32)],
        scratch_shapes=[
            pltpu.VMEM((d, 3 * hd), BF16), head, head, head, flat, flat, flat,
            pltpu.VMEM((nb, 8, BLK), F32), head, pltpu.VMEM((nc, 2 * rows, hd), BF16), flat,
            pltpu.VMEM((nb, BLK, BLK), F32),
            pltpu.VMEM((2, 4, 4, rows // 4, d), BF16),
            pltpu.VMEM((2, d, hd), BF16),
            pltpu.VMEM((nc, 2, rows, 2 * hd), F32),
            pltpu.VMEM((nc, rows, 2 * hd), F32),
            pltpu.VMEM((nc, rows, 2 * hd), F32),
            pltpu.VMEM((n, rows, 2 * hd), BF16),
            pltpu.VMEM((nc, 2 * rows, hd), BF16),
            pltpu.VMEM((n, 4, rows // 4, d // n), BF16),
            dma, dma((2, nm)), dma((2, nm)), dma((2,)),
            dma, dma((2, nm)), dma((2, nm)), dma((2,)),
            dma, dma((2, nm)),
            dma((2,)), dma, dma((2,)), dma((2, nc)), dma((2, nc)), dma((2, nc)), dma((2, nc)), dma((2,)), dma((2,)),
        ],
        compiler_params=pltpu.CompilerParams(collective_id=0, has_side_effects=True, vmem_limit_bytes=67043328),
        cost_estimate=pl.CostEstimate(flops=10**11, bytes_accessed=6 * t * d, transcendentals=t * t),
        name="mqa_backward",
    )(x.reshape(4, rows // 4, d), dy.reshape(4, rows // 4, d), wq.reshape(4, d // 4, hd), wk, wv, wo)


def solution(mesh):
    tok_spec = P(("data", "model"), None)
    n = mesh.shape["model"]

    def local_step(x_loc, dy_loc, wq_loc, w_key, w_value, wo_loc):
        d, hd = w_key.shape
        scale = 1.0 / math.sqrt(hd)
        _, _, _, dx, dwq, dwk, dwv, dwo = _step(
            x_loc, dy_loc, wq_loc.reshape(d, hd), w_key, w_value, wo_loc.reshape(hd, d), n, scale)
        return (dx, dwq[:, None, :], dwk, dwv, dwo[None])

    return jax.shard_map(
        local_step, mesh=mesh,
        in_specs=(tok_spec, tok_spec, P(None, "model", None), P(None, None), P(None, None), P("model", None, None)),
        out_specs=(tok_spec, P("data", "model", None), tok_spec, tok_spec, P(("data", "model"), None, None)),
        check_vma=False)
```

time: 932 us -> 391 us (0.42)
  waiting for transfers between devices: 621 us -> 0 us
  Pallas kernels: 0 us -> 381 us
  matrix products: 255 us -> 0 us
  other arithmetic: 21.7 us -> 0 us
  between operations: 14.4 us -> 0.66 us
    reduce_scatter x5 -> x0, waiting for transfers between devices: 424 us -> none  [the longest x1 288 us: local_step(): dx_sum = lax.psum_scatter(dx_part, 'model', scatter_dimension=0, tiled=True)]
    pallas_call x0 -> x1, Pallas kernels: none -> 381 us  [_step(): pl.pallas_call(functools.partial(_step_kernel, n, scale), in_specs=[hbm,...]
    dot_general x17 -> x0, matrix products: 255 us -> none  [the longest x1 42.6 us: local_step(): jnp.einsum('qhe,ke->hqk', d_attn, values_all, preferred_element_type=jnp....]
    all_gather x4 -> x0, waiting for transfers between devices: 196 us -> none  [the longest x1 108 us: local_step(): x_full = lax.all_gather(x_loc, 'model', axis=0, tiled=True)]
    reduce_sum x1 -> x0, other arithmetic: 21.7 us -> none  [local_step(): probs_f32 = jax.nn.softmax(scores, axis=-1)]
  transfers between devices with their start and end apart: 9 -> 0, of which waited for: 6 -> 0; matrix products, arithmetic and copies ran while one was open for 31% -> 0% of each run, Pallas kernels for 0% -> 0%
where the time goes in v2:
time: 391 us; the launch traced here: 388 us
  Pallas kernels  381 us (97%)
  local copies, waits for them, and re-layouts  6.35 us (2%)
    pallas_call x1, Pallas kernels, _step(): pl.pallas_call(functools.partial(_step_kernel, n, scale), in_specs=[hbm,...  381 us

profile of v2, /device:TPU:97, one launch (start us, length us, event | category | flops | bytes accessed | tf_op | source)
XLA Modules:
  0.0 388.3 jit_solution(8833620601163074398)
XLA Ops:
  0.6 381.2 %mqa_backward.1 = (bf16[32,4,32,4096]{3,2,1,0:T(8,128)(2,1)}, bf16[32,4,32,4096]{3,2,1,0:T(8,128)(2,1)}, bf16[32,4,1024,128]{3,2,1,0:T(8,128)(2,1)}, bf16[128,40...) custom-call(bf16[4,32,4096]{2,1,0:T(8,128)(2,1)} %bitcast.10, ...), custom_call_target="tpu_custom_call" | custom-call | flops 99999997952 | bytes 100663296 | tf_op jit(solution)/shard_map/mqa_backward/pallas_call | solution.py:554
  381.9 0.0 copy-start.1
  381.9 2.4 copy.17
  384.3 0.0 copy-done.1
  384.3 0.0 copy-start.3
  384.3 0.0 copy-start.2
  384.3 0.0 copy-start
  384.3 1.3 copy.18
  385.7 0.0 copy-done.3
  385.7 0.6 copy.19
  386.3 0.0 copy-done.2
  386.3 0.6 copy.20
  386.9 0.0 copy-done
  386.9 1.3 copy.21
Async XLA Ops:
  381.9 2.4 copy-start.1
  384.3 1.3 copy-start.3
  384.3 2.0 copy-start.2
  384.3 2.6 copy-start

commit v3 on v2

--- a/solution.py
+++ b/solution.py
@@ -172,13 +172,17 @@
             self.handed.append(m)
 
     def start(self):
-        for kind in ("S1", "S2"):
-            for part in (0, 1):
-                for s in (1, -1):
-                    self.send(part, kind, 0, s)
+        for part in (0, 1):
+            for s in (1, -1):
+                self.send(part, "S1", 0, s)
         if self.own:
             self.own.start()
         self.mine.start()
+
+    def start_cross(self):
+        for part in (0, 1):
+            for s in (1, -1):
+                self.send(part, "S2", 0, s)
 
     def first(self):
         for s in (1, -1):
@@ -212,14 +216,21 @@
             self.piece(m, self.d_sem).wait_recv()
         self.handed_in = []
 
-    def inner_ready(self):
+    def near_ready(self):
         self.mine.wait()
         if self.own:
             self.own.wait_recv()
-            for part in (0, 1):
-                for m in self.msgs:
-                    if m[0] != "F2":
-                        self.piece((part, *m), self.d_sem).wait_recv()
+            self.ready(lambda m: m[0] == "S1" or (m[0] == "S2" and m[1] != 2))
+
+    def far_ready(self):
+        if self.own:
+            self.ready(lambda m: m[0] == "F1" or (m[0] == "S2" and m[1] == 2))
+
+    def ready(self, which):
+        for part in (0, 1):
+            for m in self.msgs:
+                if which(m):
+                    self.piece((part, *m), self.d_sem).wait_recv()
 
     def finish(self):
         for m in self.sent:
@@ -231,10 +242,10 @@
 
 
 def _step_kernel(n, scale, x_ref, dy_ref, wq_ref, wk_ref, wv_ref, wo_ref,
-                 xf_ref, dyf_ref, wqf_ref, dx_ref, dwq_ref, dwk_ref, dwv_ref, dwo_ref,
-                 w3_ref, q_ref, k_ref, v_ref, kt_ref, vt_ref, ot_ref, st_ref, do_ref, dq_ref, dqt_ref, s_ref, buf, wbuf,
-                 dkv_ref, pbuf, rbuf, all_ref, dqa_ref, xc_ref,
-                 xl, xi, xd, xo, yl, yi, yd, yo, wl, wi, b_sem, c_sem, p_sem, q_sem, r_sem, g_sem, f_sem, e_sem, a_sem):
+                 xf_ref, dyf_ref, wqf_ref, dx_ref, dwq_out, dwk_ref, dwv_ref, dwo_out,
+                 w3_ref, wov_ref, q_ref, k_ref, v_ref, kt_ref, vt_ref, ot_ref, st_ref, do_ref, dq_ref, dqt_ref, s_ref, buf, wbuf,
+                 dkv_ref, pbuf, r1_ref, r2_ref, acc_ref, all_ref, dqa_ref, xc_ref, dwq_ref, dwo_ref,
+                 xl, xi, xd, xo, yl, yi, yd, yo, wl, wi, b_sem, w_sem, c_sem, p_sem, q_sem, r1_sem, r2_sem, g1_sem, g2_sem, f_sem, a_sem, o_sem):
     gx = _TorusGather(n, x_ref, xf_ref, xl, xi, xd, xo)
     gy = _TorusGather(n, dy_ref, dyf_ref, yl, yi, yd, yo)
     gw = _TorusGather(n, wq_ref, wqf_ref, wl, wi)
@@ -265,6 +276,15 @@
     pl.semaphore_wait(barrier, nc)
 
     gx.start()
+    weights = [
+        pltpu.make_async_copy(wq_ref.reshape(d, hd), w3_ref.at[:, pl.ds(0, hd)], w_sem.at[0]),
+        pltpu.make_async_copy(wk_ref, w3_ref.at[:, pl.ds(hd, hd)], w_sem.at[1]),
+        pltpu.make_async_copy(wv_ref, w3_ref.at[:, pl.ds(2 * hd, hd)], w_sem.at[2]),
+        pltpu.make_async_copy(wo_ref, wov_ref, w_sem.at[3]),
+    ]
+    for w in weights:
+        w.start()
+    gx.start_cross()
 
     def near(k):
         return gx.chip_at(lax.rem(k, 3) - 1, k // 3 - 1)
@@ -278,64 +298,81 @@
     def rows_of(c):
         return pl.ds(pl.multiple_of(c * rows, rows), rows)
 
+    def load_chip(src_ref, c, slot):
+        return [pltpu.make_async_copy(src_ref.at[2 * c + u], buf.at[slot, u], b_sem.at[slot, u]) for u in (0, 1)]
+
     def over_near(src_ref, work):
         def load(k):
-            slot = lax.rem(k, 2)
-            return pltpu.make_async_copy(src_ref.at[pl.ds(2 * near(k), 2)], buf.at[slot, pl.ds(0, 2)], b_sem.at[slot])
-
-        load(0).start()
+            return load_chip(src_ref, near(k), lax.rem(k, 2))
+
+        for cp in load(0):
+            cp.start()
 
         @pl.loop(0, 9)
         def _(k):
-            load(k).wait()
+            for cp in load(k):
+                cp.wait()
 
             @pl.when(k + 1 < 9)
             def _():
-                load(k + 1).start()
-
-            work(buf[lax.rem(k, 2), 0:2].reshape(rows, d), rows_of(near(k)))
-
-    def over_far(g, src_ref, work):
+                for cp in load(k + 1):
+                    cp.start()
+
+            work(lax.rem(k, 2), near(k))
+
+    def over_far(g, src_ref, work, hook=None):
+        def load(k):
+            return load_chip(src_ref, far(k), lax.rem(k, 2))
+
         @pl.loop(0, 7)
         def _(k):
             for z in range(4):
                 @pl.when(k == 2 * z)
                 def _():
+                    if z == 3 and hook is not None:
+                        hook()
                     g.last(z)
-
-            load = pltpu.make_async_copy(src_ref.at[pl.ds(2 * far(k), 2)], buf.at[0, pl.ds(0, 2)], b_sem.at[0])
-            load.start()
-            load.wait()
-            work(buf[0, 0:2].reshape(rows, d), rows_of(far(k)))
-
-    def project(block, here):
-        r = _dot(block, w3_ref[...]).astype(BF16)
+                    for cp in load(k):
+                        cp.start()
+                    if z < 3:
+                        for cp in load(k + 1):
+                            cp.start()
+
+            for cp in load(k):
+                cp.wait()
+            work(lax.rem(k, 2), far(k))
+
+    def project(slot, c):
+        here = rows_of(c)
+        r = _dot(buf[slot, 0:2].reshape(rows, d), w3_ref[...]).astype(BF16)
         q_ref[here, :] = r[:, :hd]
         k_ref[here, :] = r[:, hd : 2 * hd]
         v_ref[here, :] = r[:, 2 * hd :]
 
-    def project_dy(block, here):
-        do_ref[here, :] = lax.dot_general(
-            block, wo_ref[...], (((1,), (1,)), ((), ())), preferred_element_type=F32).astype(BF16)
-
-    w3_ref[:, 0:hd] = wq_ref[...].reshape(d, hd)
-    w3_ref[:, hd : 2 * hd] = wk_ref[...]
-    w3_ref[:, 2 * hd :] = wv_ref[...]
+    def project_dy(slot, c):
+        do_ref[rows_of(c), :] = lax.dot_general(
+            buf[slot, 0:2].reshape(rows, d), wov_ref[...], (((1,), (1,)), ((), ())),
+            preferred_element_type=F32).astype(BF16)
+
     dkv_ref[...] = jnp.zeros_like(dkv_ref)
+    dwo_ref[...] = jnp.zeros_like(dwo_ref)
 
     gx.first()
+    for w in weights:
+        w.wait()
     gx.second()
     for k in range(8):
         gx.third(k)
     gy.start()
-    gx.inner_ready()
+    gx.near_ready()
     over_near(xf_ref, project)
+    gy.start_cross()
+    gx.far_ready()
+    over_far(gx, xf_ref, project)
     gy.first()
-    over_far(gx, xf_ref, project)
-    gy.second()
-    cols = pltpu.make_async_copy(
+    own_cols = pltpu.make_async_copy(
         xf_ref.at[:, :, :, pl.ds(pl.multiple_of(me * (d // n), d // n), d // n)], xc_ref, c_sem)
-    cols.start()
+    own_cols.start()
 
     @pl.loop(0, nb)
     def _(j):
@@ -345,70 +382,97 @@
 
     @pl.loop(0, nb)
     def _(i):
-        for k in range(8):
-            @pl.when(i == k)
-            def _():
-                gy.third(k)
+        @pl.when(i == 5)
+        def _():
+            gy.third(0)
+            gy.third(1)
 
         _fwd_block(scale, i, q_ref, k_ref, vt_ref, ot_ref, st_ref, s_ref)
 
+    gy.second()
+    for k in range(2, 6):
+        gy.third(k)
     gw.start()
-    gy.inner_ready()
+    gy.near_ready()
     over_near(dyf_ref, project_dy)
-    over_far(gy, dyf_ref, project_dy)
+    gy.third(6)
+    gy.third(7)
+    gw.start_cross()
+    gy.far_ready()
+    over_far(gy, dyf_ref, project_dy, gw.first)
 
     @pl.loop(0, nb)
     def _(i):
-        @pl.when(i == 4)
+        @pl.when(i == 5)
         def _():
-            gw.first()
-
-        @pl.when(i == 6)
-        def _():
-            gw.second()
+            gw.third(0)
+            gw.third(1)
 
         _bwd_block(scale, i, q_ref, do_ref, ot_ref, st_ref, k_ref, v_ref, kt_ref, dq_ref, dqt_ref, dkv_ref)
 
     pair = remote(dkv_ref.at[:, 1 - core], pbuf, (p_sem.at[0], p_sem.at[1]), partner)
     pair.start()
+    dqa_ref[chip] = dq_ref[chip]
+    pair.wait()
+    side = gx.side
+    here = (gx.cx, gx.cy)
+    lanes = (pl.ds(0, hd), pl.ds(hd, hd))
+    psum = pbuf.reshape(side, side, per, 2 * hd)
+
+    @pl.loop(0, nc)
+    def _(t):
+        pbuf[t] += dkv_ref[t, core]
+
+    def sems(ref, part, o):
+        return ref.at[0, part, o], ref.at[1, part, o]
+
+    def r1_copy(part, o):
+        to = lax.rem(here[part] + o, side)
+        src = psum.at[:, to, :, lanes[part]] if part == 0 else psum.at[to, :, :, lanes[part]]
+        return remote(src, r1_ref.at[part, o], sems(r1_sem, part, o), gx.device(part, o, 0))
+
+    def r2_copy(part, o):
+        to = lax.rem(here[1 - part] + o, side)
+        return remote(acc_ref.at[part, to], r2_ref.at[part, o], sems(r2_sem, part, o), gx.device(part, 0, o))
+
+    def g1_copy(part, o):
+        ref = all_ref.at[me, :, lanes[part]]
+        return remote(ref, ref, sems(g1_sem, part, o), gx.device(part, o, 0))
+
+    def g2_copy(part, o):
+        whole = all_ref.reshape(side, side, 2, per, 2 * hd)
+        ref = whole.at[gx.cy, :, core, :, lanes[0]] if part == 0 else whole.at[:, gx.cx, core, :, lanes[1]]
+        return remote(ref, ref, sems(g2_sem, part, o), gx.device(part, 0, o))
+
+    def each(make, act):
+        for part in (0, 1):
+            for o in range(1, side):
+                getattr(make(part, o), act)()
 
     def q_copy(o):
         return remote(dq_ref.at[lax.rem(chip + o, nc)], dqa_ref.at[chip], (q_sem.at[0, o], q_sem.at[1, o]), peer(o))
 
-    @pl.loop(1, nc)
-    def _(o):
-        q_copy(o).start()
-
-    dqa_ref[chip] = dq_ref[chip]
-    gw.third(0)
-    gw.third(1)
-    pair.wait()
-
-    def r_copy(o):
-        return remote(pbuf.at[lax.rem(chip + o, nc)], rbuf.at[o], (r_sem.at[0, o], r_sem.at[1, o]), peer(o))
-
-    @pl.loop(1, nc)
-    def _(o):
-        t = lax.rem(chip + o, nc)
-        pbuf[t] += dkv_ref[t, core]
-        r_copy(o).start()
-
-    rbuf[0] = pbuf[chip] + dkv_ref[chip, core]
+    each(r1_copy, "start")
+    gw.second()
 
     def over_blocks(src_ref, work, pump):
         def load(j):
             slot = lax.rem(j, 2)
-            return pltpu.make_async_copy(src_ref.at[pl.ds(4 * j, 4)], buf.at[slot], b_sem.at[slot])
-
-        load(0).start()
+            return [pltpu.make_async_copy(
+                src_ref.at[pl.ds(4 * j + 2 * u, 2)], buf.at[slot, pl.ds(2 * u, 2)], b_sem.at[slot, u]) for u in (0, 1)]
+
+        for cp in load(0):
+            cp.start()
 
         @pl.loop(0, nb)
         def _(j):
-            load(j).wait()
+            for cp in load(j):
+                cp.wait()
 
             @pl.when(j + 1 < nb)
             def _():
-                load(j + 1).start()
+                for cp in load(j + 1):
+                    cp.start()
 
             for at, ks in pump.items():
                 @pl.when(j == at)
@@ -418,101 +482,114 @@
 
             @pl.loop(0, nb)
             def _(c):
-                work(j, c, buf[lax.rem(j, 2), :, :, :, pl.ds(pl.multiple_of(c * BLK, BLK), BLK)].reshape(BLK, BLK))
-
-    def out_grad(j, c, block):
-        here = pl.ds(pl.multiple_of(c * BLK, BLK), BLK)
-        r = _dot(ot_ref[j], block)
-        dwo_ref[:, here] = jnp.where(j == 0, r, dwo_ref[:, here] + r)
-
-    def query_grad(j, c, block):
-        r = _dot(dqt_ref[j], block)
-        s_ref[c, 3 * hd : 4 * hd] = jnp.where(j == 0, r, s_ref[c, 3 * hd : 4 * hd] + r)
-
-    dwo_ref[...] = jnp.zeros_like(dwo_ref)
+                cols = pl.ds(pl.multiple_of(c * BLK, BLK), BLK)
+                work(j, c, cols, buf[lax.rem(j, 2), :, :, :, cols].reshape(BLK, BLK))
+
+    def out_grad(j, c, at, block):
+        dwo_ref[:, at] += _dot(ot_ref[j], block)
+
+    def query_grad(j, c, at, block):
+        s_ref[c, 3 * hd : 4 * hd] += _dot(dqt_ref[j], block)
+
     s_ref[:, 3 * hd : 4 * hd] = jnp.zeros((nb, hd, BLK), F32)
-    over_blocks(dyf_ref, out_grad, {0: (2, 3), 4: (4, 5), 7: (6, 7)})
+    s_ref[:, 0:rows] = jnp.zeros((nb, rows, BLK), F32)
+    over_blocks(dyf_ref, out_grad, {0: (2, 3), 3: (4, 5)})
+    out_store = pltpu.make_async_copy(dwo_ref, dwo_out, o_sem.at[0])
+    out_store.start()
+    each(r1_copy, "wait")
+    for z in range(side):
+        for part in (0, 1):
+            got = psum[z, gx.cx, :, 0:hd] if part == 0 else psum[gx.cy, z, :, hd:]
+            for o in range(1, side):
+                got = got + r1_ref[part, o, z]
+            acc_ref[part, z] = got
+    each(r2_copy, "start")
 
     @pl.loop(1, nc)
     def _(o):
-        r_copy(o).wait()
-        rbuf[0] += rbuf[o]
-
-    all_ref[me] = rbuf[0].astype(BF16)
-
-    def g_copy(o):
-        return remote(all_ref.at[me], all_ref.at[me], (g_sem.at[0, o], g_sem.at[1, o]), peer(o))
-
-    def f_copy(o):
-        src = lax.rem(chip + nc - o, nc) * 2 + core
-        return remote(all_ref.at[src], all_ref.at[src], (f_sem.at[0, o], f_sem.at[1, o]), partner)
-
-    own = remote(all_ref.at[me], all_ref.at[me], (e_sem.at[0], e_sem.at[1]), partner)
-
-    @pl.loop(1, nc)
-    def _(o):
-        g_copy(o).start()
-
-    own.start()
-    over_blocks(xf_ref, query_grad, {})
+        q_copy(o).start()
+
+    over_blocks(xf_ref, query_grad, {2: (6, 7)})
+    each(r2_copy, "wait")
+    for part in (0, 1):
+        got = acc_ref[part, here[1 - part]]
+        for o in range(1, side):
+            got = got + r2_ref[part, o]
+        all_ref[me, :, part * hd : (part + 1) * hd] = got.astype(BF16)
+    each(g1_copy, "start")
 
     @pl.loop(0, nb)
     def _(c):
         dwq_ref[pl.ds(pl.multiple_of(c * BLK, BLK), BLK), :] = jnp.transpose(s_ref[c, 3 * hd : 4 * hd])
 
+    query_store = pltpu.make_async_copy(dwq_ref, dwq_out, o_sem.at[1])
+    query_store.start()
+    each(g1_copy, "wait")
+    each(g2_copy, "start")
+
     @pl.loop(1, nc)
     def _(o):
         q_copy(o).wait()
 
-    gw.inner_ready()
     both = (((1,), (1,)), ((), ()))
 
     def chip_of(k):
         return jnp.where(k < 9, near(k), far(k - 9))
 
     def add_heads(z):
-        c0, c1 = chip_of(2 * z), chip_of(2 * z + 1)
-        a = jnp.concatenate([dqa_ref[c0], dqa_ref[c1]], axis=1)
+        a = jnp.concatenate([dqa_ref[chip_of(2 * z)], dqa_ref[chip_of(2 * z + 1)]], axis=1)
 
         @pl.loop(0, nb)
         def _(c):
             here = pl.ds(pl.multiple_of(c * BLK, BLK), BLK)
-            w = jnp.concatenate([wbuf[0, here, :], wbuf[1, here, :]], axis=1)
-            r = lax.dot_general(a, w, both, preferred_element_type=F32)
-            s_ref[c, 0:rows] = jnp.where(z == 0, r, s_ref[c, 0:rows] + r)
-
-    s_ref[:, 0:rows] = jnp.zeros((nb, rows, BLK), F32)
-
-    @pl.loop(0, 8)
+            slot = lax.rem(z, 2)
+            w = jnp.concatenate([wbuf[slot, 0, here, :], wbuf[slot, 1, here, :]], axis=1)
+            s_ref[c, 0:rows] += lax.dot_general(a, w, both, preferred_element_type=F32)
+
+    def load_heads(z):
+        return [pltpu.make_async_copy(
+            wqf_ref.at[2 * chip_of(2 * z + u) + core], wbuf.at[lax.rem(z, 2), u].reshape(wq_ref.shape),
+            b_sem.at[lax.rem(z, 2), u]) for u in (0, 1)]
+
+    gw.near_ready()
+    for cp in load_heads(0):
+        cp.start()
+
+    @pl.loop(0, 4)
+    def _(z):
+        for cp in load_heads(z):
+            cp.wait()
+
+        @pl.when(z + 1 < 4)
+        def _():
+            for cp in load_heads(z + 1):
+                cp.start()
+
+        add_heads(z)
+
+    each(g2_copy, "wait")
+    hand_all = remote(all_ref.reshape(nc, 2, per, 2 * hd).at[:, core], all_ref.reshape(nc, 2, per, 2 * hd).at[:, core],
+                      (f_sem.at[0], f_sem.at[1]), partner)
+    hand_all.start()
+
+    @pl.loop(4, 8)
     def _(z):
         for f in range(4):
             @pl.when(z == 4 + f)
             def _():
                 gw.last(f)
 
-        for u in (0, 1):
-            pltpu.make_async_copy(
-                wqf_ref.at[2 * chip_of(2 * z + u) + core], wbuf.at[u].reshape(wq_ref.shape), b_sem.at[u]).start()
-        for u in (0, 1):
-            pltpu.make_async_copy(
-                wqf_ref.at[2 * chip_of(2 * z + u) + core], wbuf.at[u].reshape(wq_ref.shape), b_sem.at[u]).wait()
+        for cp in load_heads(z):
+            cp.start()
+        for cp in load_heads(z):
+            cp.wait()
         add_heads(z)
 
     swap = remote(s_ref.at[:, pl.ds(pl.multiple_of((1 - core) * per, per), per)], s_ref.at[:, pl.ds(rows, per)],
                   (a_sem.at[0], a_sem.at[1]), partner)
     swap.start()
-
-    @pl.loop(1, nc)
-    def _(o):
-        g_copy(o).wait()
-        f_copy(o).start()
-
-    own.wait()
-    cols.wait()
-
-    @pl.loop(1, nc)
-    def _(o):
-        f_copy(o).wait()
+    hand_all.wait()
+    own_cols.wait()
 
     def key_grad(j, acc):
         xt = _flip(xc_ref[pl.ds(4 * j, 4)].reshape(BLK, d // n)).astype(BF16)
@@ -527,14 +604,15 @@
     @pl.loop(0, nb)
     def _(c):
         here = pl.ds(pl.multiple_of(c * BLK, BLK), BLK)
-        w = jnp.concatenate([wk_ref[here, :], wv_ref[here, :]], axis=1)
-        r = lax.dot_general(mine, w, both, preferred_element_type=F32)
+        r = lax.dot_general(mine, w3_ref[here, hd:], both, preferred_element_type=F32)
         at = pl.ds(pl.multiple_of(core * per, per), per)
         dx_ref[:, here] = (s_ref[c, at] + s_ref[c, rows : rows + per] + r).astype(BF16)
 
     gx.finish()
     gy.finish()
     gw.finish()
+    out_store.wait()
+    query_store.wait()
 
 
 def _step(x, dy, wq, wk, wv, wo, n, scale):
@@ -553,29 +631,30 @@
     flat = pltpu.VMEM((nb, hd, BLK), BF16)
     return pl.pallas_call(
         functools.partial(_step_kernel, n, scale),
-        in_specs=[hbm, hbm] + [vmem] * 4,
-        out_specs=[hbm] * 3 + [vmem] * 5,
+        in_specs=[hbm] * 6,
+        out_specs=[hbm] * 3 + [vmem, hbm, vmem, vmem, hbm],
         out_shape=[
             full, full, jax.ShapeDtypeStruct((n, 4, d // 4, hd), BF16),
             jax.ShapeDtypeStruct((rows, d), BF16), jax.ShapeDtypeStruct((d, hd), F32),
             jax.ShapeDtypeStruct((d // n, hd), F32), jax.ShapeDtypeStruct((d // n, hd), F32),
             jax.ShapeDtypeStruct((hd, d), F32)],
         scratch_shapes=[
-            pltpu.VMEM((d, 3 * hd), BF16), head, head, head, flat, flat, flat,
+            pltpu.VMEM((d, 3 * hd), BF16), pltpu.VMEM((hd, d), BF16), head, head, head, flat, flat, flat,
             pltpu.VMEM((nb, 8, BLK), F32), head, pltpu.VMEM((nc, 2 * rows, hd), BF16), flat,
             pltpu.VMEM((nb, BLK, BLK), F32),
             pltpu.VMEM((2, 4, 4, rows // 4, d), BF16),
-            pltpu.VMEM((2, d, hd), BF16),
+            pltpu.VMEM((2, 2, d, hd), BF16),
             pltpu.VMEM((nc, 2, rows, 2 * hd), F32),
             pltpu.VMEM((nc, rows, 2 * hd), F32),
-            pltpu.VMEM((nc, rows, 2 * hd), F32),
+            pltpu.VMEM((2, 4, 4, rows, hd), F32), pltpu.VMEM((2, 4, rows, hd), F32), pltpu.VMEM((2, 4, rows, hd), F32),
             pltpu.VMEM((n, rows, 2 * hd), BF16),
             pltpu.VMEM((nc, 2 * rows, hd), BF16),
             pltpu.VMEM((n, 4, rows // 4, d // n), BF16),
+            pltpu.VMEM((d, hd), F32), pltpu.VMEM((hd, d), F32),
             dma, dma((2, nm)), dma((2, nm)), dma((2,)),
             dma, dma((2, nm)), dma((2, nm)), dma((2,)),
             dma, dma((2, nm)),
-            dma((2,)), dma, dma((2,)), dma((2, nc)), dma((2, nc)), dma((2, nc)), dma((2, nc)), dma((2,)), dma((2,)),
+            dma((2, 2)), dma((4,)), dma, dma((2,)), dma((2, nc)), *[dma((2, 2, 4))] * 4, dma((2,)), dma((2,)), dma((2,)),
         ],
         compiler_params=pltpu.CompilerParams(collective_id=0, has_side_effects=True, vmem_limit_bytes=67043328),
         cost_estimate=pl.CostEstimate(flops=10**11, bytes_accessed=6 * t * d, transcendentals=t * t),

time: 391 us -> 337 us (0.86)
  Pallas kernels: 381 us -> 329 us
    pallas_call x1, Pallas kernels: 381 us -> 329 us  [_step(): pl.pallas_call(functools.partial(_step_kernel, n, scale), in_specs=[hbm]...]
where the time goes in v3:
time: 337 us; the launch traced here: 336 us
  Pallas kernels  329 us (98%)
  local copies, waits for them, and re-layouts  6.35 us (2%)
    pallas_call x1, Pallas kernels, _step(): pl.pallas_call(functools.partial(_step_kernel, n, scale), in_specs=[hbm]...  329 us

profile of v3, /device:TPU:97, one launch (start us, length us, event | category | flops | bytes accessed | tf_op | source)
XLA Modules:
  0.0 335.9 jit_solution(9358894089263006405)
XLA Ops:
  0.6 328.9 %mqa_backward.1 = (bf16[32,4,32,4096]{3,2,1,0:T(8,128)(2,1)}, bf16[32,4,32,4096]{3,2,1,0:T(8,128)(2,1)}, bf16[32,4,1024,128]{3,2,1,0:T(8,128)(2,1)}, bf16[128,40...) custom-call(bf16[4,32,4096]{2,1,0:T(8,128)(2,1)} %bitcast.10, ...), custom_call_target="tpu_custom_call" | custom-call | flops 99999997952 | bytes 100663296 | tf_op jit(solution)/shard_map/mqa_backward/pallas_call | solution.py:632
  329.5 0.0 copy-start.1
  329.6 2.4 copy.17
  332.0 0.0 copy-done.1
  332.0 0.0 copy-start.3
  332.0 0.0 copy-start.2
  332.0 0.0 copy-start
  332.0 1.3 copy.18
  333.3 0.0 copy-done.3
  333.3 0.6 copy.19
  334.0 0.0 copy-done.2
  334.0 0.6 copy.20
  334.6 0.0 copy-done
  334.6 1.3 copy.21
Async XLA Ops:
  329.5 2.4 copy-start.1
  332.0 1.3 copy-start.3
  332.0 2.0 copy-start.2
  332.0 2.6 copy-start

commit v4 on v3

--- a/solution.py
+++ b/solution.py
@@ -517,6 +517,8 @@
             got = got + r2_ref[part, o]
         all_ref[me, :, part * hd : (part + 1) * hd] = got.astype(BF16)
     each(g1_copy, "start")
+    gx.finish()
+    gy.finish()
 
     @pl.loop(0, nb)
     def _(c):
@@ -524,8 +526,6 @@
 
     query_store = pltpu.make_async_copy(dwq_ref, dwq_out, o_sem.at[1])
     query_store.start()
-    each(g1_copy, "wait")
-    each(g2_copy, "start")
 
     @pl.loop(1, nc)
     def _(o):
@@ -555,36 +555,41 @@
     for cp in load_heads(0):
         cp.start()
 
-    @pl.loop(0, 4)
-    def _(z):
-        for cp in load_heads(z):
-            cp.wait()
-
-        @pl.when(z + 1 < 4)
-        def _():
-            for cp in load_heads(z + 1):
-                cp.start()
-
-        add_heads(z)
-
+    def over_heads(lo, hi, hook=None):
+        @pl.loop(lo, hi)
+        def _(z):
+            for cp in load_heads(z):
+                cp.wait()
+
+            @pl.when(z + 1 < hi)
+            def _():
+                for cp in load_heads(z + 1):
+                    cp.start()
+
+            add_heads(z)
+            if hook is not None:
+                @pl.when(z == lo + 1)
+                def _():
+                    hook()
+
+    def spread():
+        each(g1_copy, "wait")
+        each(g2_copy, "start")
+
+    over_heads(0, 4, spread)
+    for f in range(3):
+        gw.last(f)
+    for cp in load_heads(4):
+        cp.start()
+    over_heads(4, 7)
     each(g2_copy, "wait")
-    hand_all = remote(all_ref.reshape(nc, 2, per, 2 * hd).at[:, core], all_ref.reshape(nc, 2, per, 2 * hd).at[:, core],
-                      (f_sem.at[0], f_sem.at[1]), partner)
+    pairs = all_ref.reshape(nc, 2, per, 2 * hd)
+    hand_all = remote(pairs.at[:, core], pairs.at[:, core], (f_sem.at[0], f_sem.at[1]), partner)
     hand_all.start()
-
-    @pl.loop(4, 8)
-    def _(z):
-        for f in range(4):
-            @pl.when(z == 4 + f)
-            def _():
-                gw.last(f)
-
-        for cp in load_heads(z):
-            cp.start()
-        for cp in load_heads(z):
-            cp.wait()
-        add_heads(z)
-
+    gw.last(3)
+    for cp in load_heads(7):
+        cp.start()
+    over_heads(7, 8)
     swap = remote(s_ref.at[:, pl.ds(pl.multiple_of((1 - core) * per, per), per)], s_ref.at[:, pl.ds(rows, per)],
                   (a_sem.at[0], a_sem.at[1]), partner)
     swap.start()
@@ -608,8 +613,6 @@
         at = pl.ds(pl.multiple_of(core * per, per), per)
         dx_ref[:, here] = (s_ref[c, at] + s_ref[c, rows : rows + per] + r).astype(BF16)
 
-    gx.finish()
-    gy.finish()
     gw.finish()
     out_store.wait()
     query_store.wait()

time: 337 us -> 327 us (0.970)
  Pallas kernels: 329 us -> 320 us
    pallas_call x1, Pallas kernels: 329 us -> 320 us  [_step(): pl.pallas_call(functools.partial(_step_kernel, n, scale), in_specs=[hbm]...]
where the time goes in v4:
time: 327 us
  Pallas kernels  320 us (98%)
  local copies, waits for them, and re-layouts  6.35 us (2%)
    pallas_call x1, Pallas kernels, _step(): pl.pallas_call(functools.partial(_step_kernel, n, scale), in_specs=[hbm]...  320 us

profile of v4, /device:TPU:97, one launch (start us, length us, event | category | flops | bytes accessed | tf_op | source)
XLA Modules:
  0.0 326.6 jit_solution(6826819758243581995)
XLA Ops:
  0.6 319.6 %mqa_backward.1 = (bf16[32,4,32,4096]{3,2,1,0:T(8,128)(2,1)}, bf16[32,4,32,4096]{3,2,1,0:T(8,128)(2,1)}, bf16[32,4,1024,128]{3,2,1,0:T(8,128)(2,1)}, bf16[128,40...) custom-call(bf16[4,32,4096]{2,1,0:T(8,128)(2,1)} %bitcast.10, ...), custom_call_target="tpu_custom_call" | custom-call | flops 99999997952 | bytes 100663296 | tf_op jit(solution)/shard_map/mqa_backward/pallas_call | solution.py:635
  320.2 0.0 copy-start.1
  320.2 2.4 copy.17
  322.7 0.0 copy-done.1
  322.7 0.0 copy-start.3
  322.7 0.0 copy-start.2
  322.7 0.0 copy-start
  322.7 1.3 copy.18
  324.0 0.0 copy-done.3
  324.0 0.6 copy.19
  324.6 0.0 copy-done.2
  324.6 0.6 copy.20
  325.3 0.0 copy-done
  325.3 1.3 copy.21
Async XLA Ops:
  320.2 2.4 copy-start.1
  322.7 1.3 copy-start.3
  322.7 2.0 copy-start.2
  322.7 2.6 copy-start
